TPU v7x, 32 devices: a whole 2x2x4 slice. The times are simulated.
32 devices in a mesh: aa: 4 (over x, core), ba: 8 (over z, y).
Axes of the slice: x: 2, y: 2, z: 4, core: 2. Of those that a mesh axis runs over, the one named last changes fastest.
Arguments:
- activations: bfloat16 [1024, 4224], P('aa', 'ba'), may hold values from -6 to 6
- out_grad: bfloat16 [1024, 4096], P('aa', 'ba'), may hold values from -0.1875 to 0.1875
- momentum: float32 [4224, 4096], P('aa', 'ba'), may hold values from -6 to 6
- weight: float32 [4224, 4096], P('aa', 'ba'), may hold values from -6 to 6
- norm_scale: float32 [], replicated, may hold values from 128.99231 to 257.98462
- step_size: float32 [], replicated, may hold values from 0.5 to 2
Outputs:
- new_weight: float32 [4224, 4096], P('aa', 'ba')
- new_momentum: float32 [4224, 4096], P('aa', 'ba')
All inputs are finite; a program needn't handle non-finite values.
Results may differ from a plain program's by a relative error of at most 0.00068.
Values may be sent and summed in bfloat16 or wider, within the bound.
A program may use at most 64 MiB of HBM per device.

v0:
```python
import functools
import math

import jax
import jax.numpy as jnp
from jax import lax
from jax.experimental import pallas as pl
from jax.experimental.pallas import tpu as pltpu
from jax.sharding import PartitionSpec as P

ROWS = 4224
COLS = 4096
MESH = pl.DeviceIdType.MESH


def inner_rows(left, right):
    return lax.dot_general(
        left, right, (((0,), (0,)), ((), ())), preferred_element_type=jnp.float32
    )


def powers_kernel(
    n, groups, x_ref, out_ref,
    panel, powers, own_power, gram, parts, from_core, from_chip,
    x_send, x_recv, y_send, y_recv, c_send, c_recv, p_send, p_recv, s_send, s_recv,
):
    rows, width = x_ref.shape
    half, share, middle = rows // 2, width // groups, n // 2
    a, b = lax.axis_index("aa"), lax.axis_index("ba")
    core_mate = a + 1 - 2 * (a % 2)
    chip_mate = (a + 2) % groups

    place = b // 2 + (b % 2) * (n - 1 - 2 * (b // 2))

    def at(position):
        position = (position + n) % n
        column = position // middle
        return 2 * (position + column * (n - 1 - 2 * position)) + column

    neighbours = (at(place + 1), at(place - 1))

    barrier = pltpu.get_barrier_semaphore()
    for d in range(2):
        pl.semaphore_signal(barrier, 1, device_id={"ba": neighbours[d]}, device_id_type=MESH)
    for mate in (core_mate, chip_mate):
        pl.semaphore_signal(barrier, 1, device_id={"aa": mate}, device_id_type=MESH)
    pl.semaphore_wait(barrier, 4)

    def hop(own, held, send, recv, d, s, k):
        target = n - 1 if s == middle else 2 * s - 1 + d
        part = pl.ds(k * half, half)
        source = own.at[part] if s == 1 else held.at[2 * s - 3 + d, part]
        return pltpu.make_async_remote_copy(
            src_ref=source, dst_ref=held.at[target, part],
            send_sem=send.at[d, s - 1, k], recv_sem=recv.at[d, s - 1, k],
            device_id={"ba": neighbours[d]}, device_id_type=MESH,
        )

    def hops(s):
        return [(k, d) for k in range(2) for d in range(2) if s < middle or k == d]

    def ring(own, held, send, recv, use):
        for s in range(1, middle + 1):
            for k, d in hops(s):
                hop(own, held, send, recv, d, s, k).wait_recv()
                if s < middle and (k, d) in hops(s + 1):
                    hop(own, held, send, recv, d, s + 1, k).start()
            use([2 * s - 1, 2 * s] if s < middle else [n - 1])

    def drain(own, held, send, recv):
        for s in range(1, middle + 1):
            for k, d in hops(s):
                hop(own, held, send, recv, d, s, k).wait_send()

    def share_rows(index):
        return pl.ds(pl.multiple_of(index * share, share), share)

    def to_mate(source, target, send, recv, mate):
        return pltpu.make_async_remote_copy(
            src_ref=source, dst_ref=target, send_sem=send, recv_sem=recv,
            device_id={"aa": mate}, device_id_type=MESH,
        )

    def core_copy(e):
        return to_mate(
            parts.at[e, pl.ds(2, 2)], from_core.at[e], c_send.at[e], c_recv.at[e], core_mate
        )

    def chip_copy(e):
        return to_mate(parts.at[e, 1], from_chip.at[e], p_send.at[e], p_recv.at[e], chip_mate)

    def share_copy(e, step):
        mine = gram.at[e, share_rows(chip_mate if step == 2 else a)]
        return to_mate(
            mine, mine, s_send.at[e, step], s_recv.at[e, step],
            chip_mate if step == 0 else core_mate,
        )

    def block(e):
        return x_ref if e == 0 else panel.at[e]

    def gram_partial(e):
        @pl.loop(0, 4)
        def _(r):
            owner = (a + (r // 2) * (1 - 2 * (a % 2)) + 2 * (r % 2)) % groups
            parts[e, r] = inner_rows(block(e)[:, share_rows(owner)], x_ref[...])

        core_copy(e).start()

    def core_sum(e):
        core_copy(e).wait_recv()
        parts[e, 1] = parts[e, 1] + from_core[e, 1]
        chip_copy(e).start()
        parts[e, 0] = parts[e, 0] + from_core[e, 0]

    def gram_share(e):
        chip_copy(e).wait_recv()
        gram[e, share_rows(a)] = (parts[e, 0] + from_chip[e]).astype(jnp.bfloat16)
        share_copy(e, 0).start()
        share_copy(e, 1).start()

    def relay(e):
        share_copy(e, 0).wait_recv()
        share_copy(e, 2).start()

    def gram_ready(e):
        share_copy(e, 1).wait_recv()
        share_copy(e, 2).wait_recv()

    def accumulate(e, source, first, start, count):
        tile = count // 3 if count % 48 == 0 else count

        @pl.loop(0, count // tile)
        def _(t):
            part = pl.ds(pl.multiple_of(start + t * tile, 16), tile)
            term = jnp.dot(source[part, :], gram[e], preferred_element_type=jnp.float32)
            if first:
                out_ref[part, :] = term
            else:
                out_ref[part, :] += term

    for k, d in hops(1):
        hop(x_ref, panel, x_send, x_recv, d, 1, k).start()
    gram_partial(0)
    core_sum(0)
    summed, shared = [0], []

    def use_block(events):
        for e in events:
            gram_partial(e)
        for e in events:
            core_sum(e)
        for e in summed:
            gram_share(e)
        for e in shared:
            relay(e)
        shared[:] = summed
        summed[:] = events

    ring(x_ref, panel, x_send, x_recv, use_block)

    for e in range(n):
        if e == n - 4:
            gram_share(n - 1)
        if e in shared:
            relay(e)
        if e == n - 1:
            relay(e)
        gram_ready(e)
        if e < n - 1:
            accumulate(e, block(e), e == 0, 0, rows)
    for k in range(2):
        accumulate(n - 1, block(n - 1), False, k * half, half)
        part = pl.ds(k * half, half)
        own_power[part, :] = out_ref[part, :].astype(jnp.bfloat16)
        for d in range(2):
            hop(own_power, powers, y_send, y_recv, d, 1, k).start()

    def power_block(e):
        return own_power if e == 0 else powers.at[e]

    accumulate(0, own_power, True, 0, rows)

    def use_power(events):
        for e in events:
            accumulate(e, power_block(e), False, 0, rows)

    ring(own_power, powers, y_send, y_recv, use_power)
    out_ref[...] = (
        3.4445 * x_ref[...].astype(jnp.float32)
        - 4.775 * own_power[...].astype(jnp.float32)
        + 2.0315 * out_ref[...]
    )
    drain(x_ref, panel, x_send, x_recv)
    drain(own_power, powers, y_send, y_recv)
    for e in range(n):
        core_copy(e).wait_send()
        chip_copy(e).wait_send()
        for step in range(3):
            share_copy(e, step).wait_send()


def fused_direction(scaled, n, groups):
    rows, width = scaled.shape
    share = width // groups
    middle = n // 2
    dma = pltpu.SemaphoreType.DMA
    return pl.pallas_call(
        functools.partial(powers_kernel, n, groups),
        out_shape=jax.ShapeDtypeStruct((rows, width), jnp.float32),
        in_specs=[pl.BlockSpec(memory_space=pltpu.VMEM)],
        out_specs=pl.BlockSpec(memory_space=pltpu.VMEM),
        scratch_shapes=[
            pltpu.VMEM((n, rows, width), jnp.bfloat16),
            pltpu.VMEM((n, rows, width), jnp.bfloat16),
            pltpu.VMEM((rows, width), jnp.bfloat16),
            pltpu.VMEM((n, width, width), jnp.bfloat16),
            pltpu.VMEM((n, 4, share, width), jnp.float32),
            pltpu.VMEM((n, 2, share, width), jnp.float32),
            pltpu.VMEM((n, share, width), jnp.float32),
            dma((2, middle, 2)), dma((2, middle, 2)),
            dma((2, middle, 2)), dma((2, middle, 2)),
            dma((n,)), dma((n,)), dma((n,)), dma((n,)),
            dma((n, 3)), dma((n, 3)),
        ],
        compiler_params=pltpu.CompilerParams(
            collective_id=0, has_side_effects=True, vmem_limit_bytes=62 * 1024 * 1024
        ),
        name="powers",
    )(scaled)


def tokens_kernel(
    n, groups, act_ref, grad_ref, act_out, grad_out,
    held, tiles, grads, h_send, h_recv, t_send, t_recv, g_send, g_recv,
):
    middle, half = n // 2, act_ref.shape[0] // 2
    a, b = lax.axis_index("aa"), lax.axis_index("ba")
    place = b // 2 + (b % 2) * (n - 1 - 2 * (b // 2))

    def at(position):
        position = (position + n) % n
        column = position // middle
        return 2 * (position + column * (n - 1 - 2 * position)) + column

    neighbours = (at(place + 1), at(place - 1))
    peers = [(a + r) % groups for r in range(groups)]
    barrier = pltpu.get_barrier_semaphore()
    for d in range(2):
        pl.semaphore_signal(barrier, 1, device_id={"ba": neighbours[d]}, device_id_type=MESH)
    for r in range(1, groups):
        pl.semaphore_signal(barrier, 1, device_id={"aa": peers[r]}, device_id_type=MESH)
    pl.semaphore_wait(barrier, groups + 1)

    def hop(d, s, k):
        target = n - 1 if s == middle else 2 * s - 1 + d
        part = pl.ds(k * half, half)
        source = act_ref.at[part] if s == 1 else held.at[2 * s - 3 + d, part]
        return pltpu.make_async_remote_copy(
            src_ref=source, dst_ref=held.at[target, part],
            send_sem=h_send.at[d, s - 1, k], recv_sem=h_recv.at[d, s - 1, k],
            device_id={"ba": neighbours[d]}, device_id_type=MESH,
        )

    def hops(s):
        return [(k, d) for k in range(2) for d in range(2) if s < middle or k == d]

    def grad_copy(r):
        return pltpu.make_async_remote_copy(
            src_ref=grad_ref, dst_ref=grads.at[a],
            send_sem=g_send.at[r], recv_sem=g_recv.at[r],
            device_id={"aa": peers[r]}, device_id_type=MESH,
        )

    def block(e):
        return act_ref if e == 0 else held.at[e]

    def owner(e):
        if e == 0:
            return b
        if e == n - 1:
            return at(place + middle)
        s = (e + 1) // 2
        return at(place - s) if e % 2 else at(place + s)

    def tile_copy(e):
        index = owner(e)
        return pltpu.make_async_remote_copy(
            src_ref=block(e), dst_ref=tiles.at[index % 2, a],
            send_sem=t_send.at[e], recv_sem=t_recv.at[index % 2, a],
            device_id={"aa": index // 2}, device_id_type=MESH,
        )

    def deliver(e):
        index = owner(e)

        @pl.when(index // 2 != a)
        def _():
            tile_copy(e).start()

        @pl.when(index // 2 == a)
        def _():
            tiles[index % 2, a] = block(e)[...]

    for k, d in hops(1):
        hop(d, 1, k).start()
    deliver(0)
    for r in range(1, groups):
        grad_copy(r).start()
    grads[a] = grad_ref[...]
    for s in range(1, middle + 1):
        for k, d in hops(s):
            hop(d, s, k).wait_recv()
            if s < middle and (k, d) in hops(s + 1):
                hop(d, s + 1, k).start()
        for e in [2 * s - 1, 2 * s] if s < middle else [n - 1]:
            deliver(e)

    for r in range(1, groups):
        grad_copy(r).wait_recv()
        for k in range(2):
            pltpu.make_async_remote_copy(
                src_ref=act_ref, dst_ref=tiles.at[k, peers[r]],
                send_sem=t_send.at[0], recv_sem=t_recv.at[k, peers[r]],
                device_id={"aa": peers[r]}, device_id_type=MESH,
            ).wait_recv()
    act_out[...] = tiles[...]
    grad_out[...] = grads[...]
    for s in range(1, middle + 1):
        for k, d in hops(s):
            hop(d, s, k).wait_send()
    for r in range(1, groups):
        grad_copy(r).wait_send()
    for e in range(n):
        @pl.when(owner(e) // 2 != a)
        def _():
            tile_copy(e).wait_send()


def kernel_gradient(activations, out_grad, n, groups):
    tokens, features = activations.shape
    width = out_grad.shape[1]
    middle = n // 2
    dma = pltpu.SemaphoreType.DMA
    vmem = pl.BlockSpec(memory_space=pltpu.VMEM)
    tiles, grads = pl.pallas_call(
        functools.partial(tokens_kernel, n, groups),
        out_shape=(
            jax.ShapeDtypeStruct((2, groups, tokens, features), jnp.bfloat16),
            jax.ShapeDtypeStruct((groups, tokens, width), jnp.bfloat16),
        ),
        in_specs=[vmem, vmem],
        out_specs=(vmem, vmem),
        scratch_shapes=[
            pltpu.VMEM((n, tokens, features), jnp.bfloat16),
            pltpu.VMEM((2, groups, tokens, features), jnp.bfloat16),
            pltpu.VMEM((groups, tokens, width), jnp.bfloat16),
            dma((2, middle, 2)), dma((2, middle, 2)),
            dma((n,)), dma((2, groups)), dma((groups,)), dma((groups,)),
        ],
        compiler_params=pltpu.CompilerParams(
            collective_id=1, has_side_effects=True, vmem_limit_bytes=48 * 1024 * 1024
        ),
        name="tokens",
    )(activations, out_grad)
    grads = grads.reshape(groups * tokens, width)
    tiles = tiles.reshape(2, groups * tokens, features)
    return jnp.concatenate([inner_rows(tiles[k], grads) for k in range(2)], axis=0)


def plain_gradient(activations, out_grad):
    features = lax.all_to_all(
        lax.all_gather(activations, "ba", axis=1, tiled=True),
        "aa", split_axis=1, concat_axis=0, tiled=True,
    )
    return inner_rows(features, lax.all_gather(out_grad, "aa", axis=0, tiled=True))


def plain_direction(scaled):
    row_panel = lax.all_gather(scaled, "ba", axis=1, tiled=True)
    gram_part = inner_rows(row_panel, scaled)
    width = gram_part.shape[0]
    groups = lax.axis_size("aa")
    padding = (groups - width % groups) % groups
    padded = jnp.pad(gram_part, ((0, padding), (0, 0)))
    share = lax.psum_scatter(padded, "aa", scatter_dimension=0, tiled=True).astype(jnp.bfloat16)
    gram_cols = lax.all_gather(share, "aa", axis=0, tiled=True)[:width]
    first_power = jnp.dot(row_panel, gram_cols, preferred_element_type=jnp.float32).astype(
        jnp.bfloat16
    )
    second_power = jnp.dot(
        lax.all_gather(first_power, "ba", axis=1, tiled=True),
        gram_cols,
        preferred_element_type=jnp.float32,
    )
    return (
        3.4445 * scaled.astype(jnp.float32)
        - 4.775 * first_power.astype(jnp.float32)
        + 2.0315 * second_power
    )


def per_device(activations, out_grad, momentum, weight, norm_scale, step_size):
    n, groups = lax.axis_size("ba"), lax.axis_size("aa")
    rows, width = momentum.shape
    fits = (
        n % 2 == 0 and n >= 4 and width % 128 == 0
        and width % (16 * groups) == 0 and rows % 32 == 0 and groups == 4
        and (width // groups) % 128 == 0
        and 4 * n * rows * width + 9 * n * width * width + 9 * rows * width < 56 * 2**20
    )
    if fits and n == 2 * groups and activations.shape[0] % 32 == 0:
        gradient = kernel_gradient(activations, out_grad, n, groups)
    else:
        gradient = plain_gradient(activations, out_grad)
    new_momentum = 0.95 * momentum + gradient
    scaled = (new_momentum / norm_scale).astype(jnp.bfloat16)
    direction = fused_direction(scaled, n, groups) if fits else plain_direction(scaled)
    factor = 0.2 * math.sqrt(max(ROWS, COLS))
    new_weight = weight - step_size * factor * direction
    return (new_weight, new_momentum)


def solution(mesh):
    placed = (P("aa", "ba"), P("aa", "ba"), P("aa", "ba"), P("aa", "ba"), P(), P())
    return jax.shard_map(
        per_device,
        mesh=mesh,
        in_specs=placed,
        out_specs=(P("aa", "ba"), P("aa", "ba")),
        check_vma=False,
    )
```

profile of v0, /device:TPU:0, one launch (start us, length us, event | category | flops | bytes accessed | tf_op | source)
XLA Modules:
  0.0 266.0 jit_solution(10235190160216804762)
XLA Ops:
  0.6 1.2 copy.8.act_ref
  1.8 0.0 copy-start
  1.8 0.9 copy-done
  2.7 48.0 %tokens.1 = (bf16[2,4,256,528]{3,2,1,0:T(8,128)(2,1)S(1)}, bf16[4,256,512]{2,1,0:T(8,128)(2,1)S(1)}) custom-call(bf16[256,528]{1,0:T(8,128)(2,1)S(1)} %copy.8.act_ref, bf16[256,512]{1,0:T(8,128)(2,1)S(1)} %copy-done), custom_call_target="tpu_custom_call" | custom-call | tf_op jit(solution)/shard_map/tokens/pallas_call | solution.py:346
  50.8 0.3 fusion
  51.1 0.8 fusion.1
  51.8 0.0 copy-start.1
  51.9 1.7 fusion.2
  54.2 0.0 copy-done.1
  54.3 3.5 %divide_convert_fusion = (bf16[1056,512]{1,0:T(8,128)(2,1)}, f32[1056,512]{1,0:T(8,128)}) fusion(f32[]{:T(128)S(6)} %copy.9, f32[528,512]{1,0:T(8,128)} %fusion.2, f32[528,512]{1,0:T(8,128)S(1)} %fusion.1, f32[1056,512]{1,0:T(8,128)S(1)} %copy-done.1), kind=kLoop, calls=%fused_computation.2 | loop fusion | flops 2703360 | bytes 7569412 | tf_op jit(solution)/shard_map/convert_element_type | solution.py:417
  57.8 203.5 %powers.1 = f32[1056,512]{1,0:T(8,128)} custom-call(bf16[1056,512]{1,0:T(8,128)(2,1)} %get-tuple-element.6.x_ref), custom_call_target="tpu_custom_call" | custom-call | tf_op jit(solution)/shard_map/powers/pallas_call | solution.py:208
  261.9 4.1 %multiply_subtract_fusion = f32[1056,512]{1,0:T(8,128)} fusion(f32[1056,512]{1,0:T(8,128)} %param.9, f32[1056,512]{1,0:T(8,128)} %powers.1, f32[]{:T(128)S(6)} %mul.15), kind=kLoop, calls=%fused_computation.1 | loop fusion | flops 1081344 | bytes 6488068 | tf_op jit(solution)/shard_map/sub | solution.py:420
Async XLA Ops:
  1.8 1.0 copy-start
  51.8 2.4 copy-start.1
where the time goes:
time: 266 us
  Pallas kernels  252 us (95%)
  other arithmetic  7.63 us (3%)
    pallas_call x1, Pallas kernels, fused_direction(): pl.pallas_call(functools.partial(powers_kernel, n, groups), out_shape=jax...  203 us
    pallas_call x1, Pallas kernels, kernel_gradient(): pl.pallas_call(functools.partial(tokens_kernel, n, groups), out_shape=(ja...  48 us

commit v1 on v0

v1 whole, which is shorter than its diff:
```python
import functools
import math

import jax
import jax.numpy as jnp
from jax import lax
from jax.experimental import pallas as pl
from jax.experimental.pallas import tpu as pltpu
from jax.sharding import PartitionSpec as P

ROWS = 4224
COLS = 4096
MESH = pl.DeviceIdType.MESH


def inner_rows(left, right):
    return lax.dot_general(
        left, right, (((0,), (0,)), ((), ())), preferred_element_type=jnp.float32
    )


def step_kernel(
    n, groups, factor,
    act_ref, grad_ref, momentum_hbm, weight_hbm, scale_ref, step_ref,
    new_weight_hbm, new_momentum_hbm,
    line, tiles, grads, panel, powers, gram, parts, from_core, from_chip,
    momentum, weight, total,
    z_send, z_recv, t_send, t_recv, g_send, g_recv,
    x_send, x_recv, y_send, y_recv, c_send, c_recv, p_send, p_recv, s_send, s_recv,
    load_sem, store_sem,
):
    half = act_ref.shape[0]
    rows, width = momentum.shape
    wide, middle, layers = width // 2, n // 2, n // 2
    core_rows, share = wide // 2, wide // groups
    row_tile = half // 3 if half % 48 == 0 else half
    a, b = lax.axis_index("aa"), lax.axis_index("ba")
    x, c, z, y = a // 2, a % 2, b // 2, b % 2
    core_mate = 2 * x + 1 - c
    chip_mate = 2 * (1 - x) + c
    y_mate = 2 * z + 1 - y

    loads = [
        pltpu.make_async_copy(momentum_hbm, momentum, load_sem.at[0]),
        pltpu.make_async_copy(weight_hbm, weight, load_sem.at[1]),
    ]
    for load in loads:
        load.start()

    place = z + y * (n - 1 - 2 * z)

    def at(position):
        position = (position + n) % n
        column = position // middle
        return 2 * (position + column * (n - 1 - 2 * position)) + column

    neighbours = (at(place + 1), at(place - 1))

    barrier = pltpu.get_barrier_semaphore()
    for r in range(1, groups):
        pl.semaphore_signal(barrier, 1, device_id={"aa": (a + r) % groups}, device_id_type=MESH)
    for r in range(groups):
        pl.semaphore_signal(
            barrier, 1, device_id={"aa": (a + r) % groups, "ba": y_mate}, device_id_type=MESH
        )

    @pl.when(z > 0)
    def _():
        pl.semaphore_signal(barrier, 1, device_id={"ba": b - 2}, device_id_type=MESH)

    @pl.when(z < layers - 1)
    def _():
        pl.semaphore_signal(barrier, 1, device_id={"ba": b + 2}, device_id_type=MESH)

    sides = (z + layers - 1) // layers + (2 * layers - 2 - z) // layers
    pl.semaphore_wait(barrier, 2 * groups - 1 + sides)

    def z_hop(source, layer, side):
        return pltpu.make_async_remote_copy(
            src_ref=source, dst_ref=line.at[layer],
            send_sem=z_send.at[side, layer], recv_sem=z_recv.at[layer],
            device_id={"ba": b + 2 - 4 * side}, device_id_type=MESH,
        )

    def near_copy(source, layer):
        return pltpu.make_async_remote_copy(
            src_ref=source, dst_ref=tiles.at[y, a],
            send_sem=t_send.at[0, layer], recv_sem=t_recv.at[y, a],
            device_id={"aa": layer}, device_id_type=MESH,
        )

    def far_copy(source, layer):
        return pltpu.make_async_remote_copy(
            src_ref=source, dst_ref=tiles.at[y, a],
            send_sem=t_send.at[1, layer], recv_sem=t_recv.at[y, a],
            device_id={"aa": layer, "ba": y_mate}, device_id_type=MESH,
        )

    def deliver(source, layer):
        far_copy(source, layer).start()

        @pl.when(layer != a)
        def _():
            near_copy(source, layer).start()

        @pl.when(layer == a)
        def _():
            tiles[y, a] = source[...]

    def grad_copy(kind):
        mate = chip_mate if kind == 0 else core_mate
        source, slot = (grads.at[chip_mate], chip_mate) if kind == 2 else (grad_ref, a)
        return pltpu.make_async_remote_copy(
            src_ref=source, dst_ref=grads.at[slot],
            send_sem=g_send.at[kind], recv_sem=g_recv.at[kind],
            device_id={"aa": mate}, device_id_type=MESH,
        )

    can_go = (z < layers - 1, z > 0)
    for side in range(2):
        pl.when(can_go[side])(z_hop(act_ref, z, side).start)
    grad_copy(0).start()
    grad_copy(1).start()
    deliver(act_ref, z)
    grads[a] = grad_ref[...]
    for distance in range(1, layers):
        for side in range(2):
            layer = z - distance if side == 0 else z + distance

            @pl.when((layer >= 0) & (layer < layers))
            def _():
                z_hop(line.at[layer], layer, side).wait_recv()
                pl.when(can_go[side])(z_hop(line.at[layer], layer, side).start)
                deliver(line.at[layer], layer)

        if distance == 1:
            grad_copy(0).wait_recv()
            grad_copy(2).start()
    grad_copy(1).wait_recv()
    grad_copy(2).wait_recv()
    for load in loads:
        load.wait()

    order = [(h, k) for k in range(2) for h in range(2)]

    def hop(held, send, recv, d, s, h, k):
        target = n - 1 if s == middle else 2 * s - 1 + d
        origin = 0 if s == 1 else 2 * s - 3 + d
        part = pl.ds(k * half, half)
        return pltpu.make_async_remote_copy(
            src_ref=held.at[origin, h, part], dst_ref=held.at[target, h, part],
            send_sem=send.at[d, s - 1, h, k], recv_sem=recv.at[d, s - 1, h, k],
            device_id={"ba": neighbours[d]}, device_id_type=MESH,
        )

    def goes(by_rows, d, s, h, k):
        return s < middle or d == (k if by_rows else h)

    def pass_on(held, send, recv, by_rows, d, s, h, k):
        hop(held, send, recv, d, s, h, k).wait_recv()
        if s < middle and goes(by_rows, d, s + 1, h, k):
            hop(held, send, recv, d, s + 1, h, k).start()

    def drain(held, send, recv, by_rows):
        for s in range(1, middle + 1):
            for h, k in order:
                for d in range(2):
                    if goes(by_rows, d, s, h, k):
                        hop(held, send, recv, d, s, h, k).wait_send()

    for k in range(2):
        for r in range(groups):
            pl.when((k != y) | (r != a))(
                pltpu.make_async_remote_copy(
                    src_ref=act_ref, dst_ref=tiles.at[k, r],
                    send_sem=t_send.at[0, 0], recv_sem=t_recv.at[k, r],
                    device_id={"aa": core_mate}, device_id_type=MESH,
                ).wait_recv
            )

        @pl.loop(0, half // row_tile)
        def _(t):
            source = pl.ds(pl.multiple_of(t * row_tile, 16), row_tile)
            part = pl.ds(pl.multiple_of(k * half + t * row_tile, 16), row_tile)
            gradient = sum(
                jnp.dot(tiles[k, r, source, :], grads[r], preferred_element_type=jnp.float32)
                for r in range(groups)
            )
            updated = 0.95 * momentum[part, :] + gradient
            momentum[part, :] = updated
            scaled = (updated / scale_ref[0]).astype(jnp.bfloat16)
            for h in range(2):
                panel[0, h, part, :] = scaled[:, h * wide : (h + 1) * wide]

        for h in range(2):
            for d in range(2):
                hop(panel, x_send, x_recv, d, 1, h, k).start()

    store_momentum = pltpu.make_async_copy(momentum, new_momentum_hbm, store_sem.at[0])
    store_momentum.start()

    def to_mate(source, target, send, recv, mate):
        return pltpu.make_async_remote_copy(
            src_ref=source, dst_ref=target, send_sem=send, recv_sem=recv,
            device_id={"aa": mate}, device_id_type=MESH,
        )

    def span(start, size):
        return pl.ds(pl.multiple_of(start, size), size)

    mine, theirs = c * core_rows + x * share, c * core_rows + (1 - x) * share

    def core_copy(e, h):
        return to_mate(
            parts.at[e, h, span((1 - c) * core_rows, core_rows)], from_core.at[e, h],
            c_send.at[e, h], c_recv.at[e, h], core_mate,
        )

    def chip_copy(e, h):
        return to_mate(
            parts.at[e, h, span(theirs, share)], from_chip.at[e, h],
            p_send.at[e, h], p_recv.at[e, h], chip_mate,
        )

    def share_copy(e, h, step):
        rows_of = gram.at[e, span(h * wide + (theirs if step == 2 else mine), share)]
        return to_mate(
            rows_of, rows_of, s_send.at[e, h, step], s_recv.at[e, h, step],
            chip_mate if step == 0 else core_mate,
        )

    def gram_partial(e, h):
        @pl.loop(0, 2)
        def _(q):
            parts[e, h, :, span(q * wide, wide)] = inner_rows(panel[e, h], panel[0, q])

        core_copy(e, h).start()

    def core_sum(e, h):
        core_copy(e, h).wait_recv()
        parts[e, h, span(theirs, share)] += from_core[e, h, span((1 - x) * share, share)]
        chip_copy(e, h).start()
        parts[e, h, span(mine, share)] += from_core[e, h, span(x * share, share)]

    def gram_share(e, h):
        chip_copy(e, h).wait_recv()
        gram[e, span(h * wide + mine, share)] = (
            parts[e, h, span(mine, share)] + from_chip[e, h]
        ).astype(jnp.bfloat16)
        share_copy(e, h, 0).start()
        share_copy(e, h, 1).start()

    def relay(e, h):
        share_copy(e, h, 0).wait_recv()
        share_copy(e, h, 2).start()

    def gram_ready(e, h):
        share_copy(e, h, 1).wait_recv()
        share_copy(e, h, 2).wait_recv()

    def accumulate(held, e, halves, first, start, count):
        @pl.loop(0, count // row_tile)
        def _(t):
            part = pl.ds(pl.multiple_of(start + t * row_tile, 16), row_tile)
            term = sum(
                jnp.dot(
                    held[e, h, part, :], gram[e, h * wide : (h + 1) * wide, :],
                    preferred_element_type=jnp.float32,
                )
                for h in halves
            )
            if first:
                total[part, :] = term
            else:
                total[part, :] += term

    summed, shared = [], []

    def advance():
        for unit in shared:
            relay(*unit)
        for unit in summed:
            gram_share(*unit)
        shared[:] = summed
        summed[:] = []

    def use_units(units):
        for unit in units:
            gram_partial(*unit)
        advance()
        for unit in units:
            core_sum(*unit)
        summed[:] = units

    ring_x = (panel, x_send, x_recv, True)
    use_units([(0, 0), (0, 1)])
    for s in range(1, middle):
        for i, (h, k) in enumerate(order):
            for d in range(2):
                pass_on(*ring_x, d, s, h, k)
            if i == 1:
                advance()
        use_units([(e, h) for h in range(2) for e in (2 * s - 1, 2 * s)])
    last = n - 1
    for h in range(2):
        for d in range(2):
            pass_on(*ring_x, d, middle, h, d)
        if h == 0:
            use_units([(last, 0)])
    gram_partial(last, 1)
    advance()
    for e in range(n):
        if e == 1:
            core_sum(last, 1)
        if e == 3:
            advance()
            summed[:] = [(last, 1)]
        if e == last - 2:
            advance()
        if e == last:
            advance()
        for h in range(2 if e < last else 1):
            gram_ready(e, h)
        accumulate(panel, e, (0, 1) if e < last else (0,), e == 0, 0, rows)
    advance()
    gram_ready(last, 1)

    ring_p = (powers, y_send, y_recv, False)
    for k in range(2):
        part = pl.ds(k * half, half)
        accumulate(panel, last, (1,), False, k * half, half)
        for h in range(2):
            powers[0, h, part, :] = total[part, h * wide : (h + 1) * wide].astype(jnp.bfloat16)
            for d in range(2):
                hop(powers, y_send, y_recv, d, 1, h, k).start()

    accumulate(powers, 0, (0, 1), True, 0, rows)
    for s in range(1, middle):
        for h, k in order:
            for d in range(2):
                pass_on(*ring_p, d, s, h, k)
        for e in (2 * s - 1, 2 * s):
            accumulate(powers, e, (0, 1), False, 0, rows)

    rate = step_ref[0] * factor
    stores = []
    for k in range(2):
        for d in range(2):
            pass_on(*ring_p, d, middle, d, k)
        accumulate(powers, last, (0, 1), False, k * half, half)
        part = pl.ds(k * half, half)
        for h in range(2):
            columns = slice(h * wide, (h + 1) * wide)
            direction = (
                3.4445 * panel[0, h, part, :].astype(jnp.float32)
                - 4.775 * powers[0, h, part, :].astype(jnp.float32)
                + 2.0315 * total[part, columns]
            )
            weight[part, columns] = weight[part, columns] - rate * direction
        stores.append(
            pltpu.make_async_copy(
                weight.at[part], new_weight_hbm.at[part], store_sem.at[1 + k]
            )
        )
        stores[-1].start()

    drain(*ring_x)
    drain(*ring_p)
    for e in range(n):
        for h in range(2):
            core_copy(e, h).wait_send()
            chip_copy(e, h).wait_send()
            for step in range(3):
                share_copy(e, h, step).wait_send()
    for kind in range(3):
        grad_copy(kind).wait_send()
    for layer in range(layers):
        far_copy(act_ref, layer).wait_send()
        pl.when(layer != a)(near_copy(act_ref, layer).wait_send)
        for side in range(2):
            from_here = layer <= z if side == 0 else layer >= z
            pl.when(from_here & can_go[side])(z_hop(act_ref, layer, side).wait_send)
    store_momentum.wait()
    for store in stores:
        store.wait()


def fused_step(activations, out_grad, momentum, weight, norm_scale, step_size, n, groups):
    tokens, features = activations.shape
    rows, width = momentum.shape
    wide, middle = width // 2, n // 2
    dma = pltpu.SemaphoreType.DMA
    vmem = pl.BlockSpec(memory_space=pltpu.VMEM)
    hbm = pl.BlockSpec(memory_space=pl.ANY)
    smem = pl.BlockSpec(memory_space=pltpu.SMEM)
    ring = dma((2, middle, 2, 2))
    units = dma((n, 2))
    return pl.pallas_call(
        functools.partial(step_kernel, n, groups, 0.2 * math.sqrt(max(ROWS, COLS))),
        out_shape=(
            jax.ShapeDtypeStruct((rows, width), jnp.float32),
            jax.ShapeDtypeStruct((rows, width), jnp.float32),
        ),
        in_specs=[vmem, vmem, hbm, hbm, smem, smem],
        out_specs=(hbm, hbm),
        scratch_shapes=[
            pltpu.VMEM((n // 2, features, tokens), jnp.bfloat16),
            pltpu.VMEM((2, groups, features, tokens), jnp.bfloat16),
            pltpu.VMEM((groups, tokens, width), jnp.bfloat16),
            pltpu.VMEM((n, 2, rows, wide), jnp.bfloat16),
            pltpu.VMEM((n, 2, rows, wide), jnp.bfloat16),
            pltpu.VMEM((n, width, width), jnp.bfloat16),
            pltpu.VMEM((n, 2, wide, width), jnp.float32),
            pltpu.VMEM((n, 2, wide // 2, width), jnp.float32),
            pltpu.VMEM((n, 2, wide // groups, width), jnp.float32),
            pltpu.VMEM((rows, width), jnp.float32),
            pltpu.VMEM((rows, width), jnp.float32),
            pltpu.VMEM((rows, width), jnp.float32),
            dma((2, n // 2)), dma((n // 2,)),
            dma((2, n // 2)), dma((2, groups)),
            dma((3,)), dma((3,)),
            ring, ring, ring, ring,
            units, units, units, units,
            dma((n, 2, 3)), dma((n, 2, 3)),
            dma((2,)), dma((3,)),
        ],
        compiler_params=pltpu.CompilerParams(
            collective_id=0, has_side_effects=True, vmem_limit_bytes=62 * 1024 * 1024
        ),
        name="step",
    )(activations.T, out_grad, momentum, weight, norm_scale.reshape(1), step_size.reshape(1))


def plain_gradient(activations, out_grad):
    features = lax.all_to_all(
        lax.all_gather(activations, "ba", axis=1, tiled=True),
        "aa", split_axis=1, concat_axis=0, tiled=True,
    )
    return inner_rows(features, lax.all_gather(out_grad, "aa", axis=0, tiled=True))


def plain_direction(scaled):
    row_panel = lax.all_gather(scaled, "ba", axis=1, tiled=True)
    gram_part = inner_rows(row_panel, scaled)
    width = gram_part.shape[0]
    groups = lax.axis_size("aa")
    padding = (groups - width % groups) % groups
    padded = jnp.pad(gram_part, ((0, padding), (0, 0)))
    share = lax.psum_scatter(padded, "aa", scatter_dimension=0, tiled=True).astype(jnp.bfloat16)
    gram_cols = lax.all_gather(share, "aa", axis=0, tiled=True)[:width]
    first_power = jnp.dot(row_panel, gram_cols, preferred_element_type=jnp.float32).astype(
        jnp.bfloat16
    )
    second_power = jnp.dot(
        lax.all_gather(first_power, "ba", axis=1, tiled=True),
        gram_cols,
        preferred_element_type=jnp.float32,
    )
    return (
        3.4445 * scaled.astype(jnp.float32)
        - 4.775 * first_power.astype(jnp.float32)
        + 2.0315 * second_power
    )


def per_device(activations, out_grad, momentum, weight, norm_scale, step_size):
    n, groups = lax.axis_size("ba"), lax.axis_size("aa")
    rows, width = momentum.shape
    tokens, features = activations.shape
    fits = (
        groups == 4 and n == 2 * groups and rows == 2 * features
        and features % 16 == 0 and tokens % 128 == 0 and width % 256 == 0
        and width % (32 * groups) == 0
        and 4 * n * rows * width + 9 * n * width * width + 17 * rows * width < 56 * 2**20
    )
    if fits:
        return fused_step(
            activations, out_grad, momentum, weight, norm_scale, step_size, n, groups
        )
    new_momentum = 0.95 * momentum + plain_gradient(activations, out_grad)
    scaled = (new_momentum / norm_scale).astype(jnp.bfloat16)
    factor = 0.2 * math.sqrt(max(ROWS, COLS))
    new_weight = weight - step_size * factor * plain_direction(scaled)
    return (new_weight, new_momentum)


def solution(mesh):
    placed = (P("aa", "ba"), P("aa", "ba"), P("aa", "ba"), P("aa", "ba"), P(), P())
    return jax.shard_map(
        per_device,
        mesh=mesh,
        in_specs=placed,
        out_specs=(P("aa", "ba"), P("aa", "ba")),
        check_vma=False,
    )
```

time: 266 us -> 252 us (0.947)
  other arithmetic: 7.63 us -> 0 us
  Pallas kernels: 252 us -> 245 us
    pallas_call x2 -> x1, Pallas kernels: 252 us -> 245 us  [fused_step(): pl.pallas_call(functools.partial(step_kernel, n, groups, 0.2 * math.sqrt(...]
    sub x1 -> x0, other arithmetic: 4.11 us -> none  [per_device(): new_weight = weight - step_size * factor * direction]
    convert_element_type x1 -> x0, other arithmetic: 3.52 us -> none  [per_device(): scaled = (new_momentum / norm_scale).astype(jnp.bfloat16)]
where the time goes in v1:
time: 252 us; the launch traced here: 251 us
  Pallas kernels  245 us (97%)
  local copies, waits for them, and re-layouts  4.62 us (2%)
    pallas_call x1, Pallas kernels, fused_step(): pl.pallas_call(functools.partial(step_kernel, n, groups, 0.2 * math.sqrt(...  245 us

profile of v1, /device:TPU:0, one launch (start us, length us, event | category | flops | bytes accessed | tf_op | source)
XLA Modules:
  0.0 251.5 jit_solution(13898795020391659385)
XLA Ops:
  1.9 244.9 %step.1 = (f32[1056,512]{1,0:T(8,128)}, f32[1056,512]{1,0:T(8,128)}) custom-call(bf16[528,256]{1,0:T(8,128)(2,1)} %bitcast.5, bf16[256,512]{1,0:T(8,128)(2,1)} %grad_ref.1, f32[1056,512]{1,0:T(8,128)} %momentum_hbm.1, f32[1056,512]{1,0:T(8,128)} %weight_hbm.1, f32[1]{0:T(128)} %bitcast.3.scale_ref, f32[1]{0:T(128)} %bitcast.4.step_ref), custom_call_target="tpu_custom_call" | custom-call | tf_op jit(solution)/shard_map/step/pallas_call | solution.py:398
  246.8 0.0 copy-start
  246.8 3.3 %copy.12 = f32[1056,512]{1,0:T(8,128)} copy(f32[1056,512]{1,0:T(8,128)} %get-tuple-element.4) | data formatting | bytes 4325376
  250.1 0.0 copy-done
  250.1 1.3 copy.13
Async XLA Ops:
  246.8 3.3 %copy-start = (f32[1056,512]{1,0:T(8,128)S(1)}, f32[1056,512]{1,0:T(8,128)}, u32[]{:S(2)}) copy-start(f32[1056,512]{1,0:T(8,128)} %get-tuple-element.5) | copy-start | bytes 6488068

commit v2 on v1

--- a/solution.py
+++ b/solution.py
@@ -22,18 +22,17 @@
 def step_kernel(
     n, groups, factor,
     act_ref, grad_ref, momentum_hbm, weight_hbm, scale_ref, step_ref,
-    new_weight_hbm, new_momentum_hbm,
-    line, tiles, grads, panel, powers, gram, parts, from_core, from_chip,
-    momentum, weight, total,
-    z_send, z_recv, t_send, t_recv, g_send, g_recv,
+    weight, momentum,
+    line, tiles, grads, panel, powers, gram, parts, from_core, from_chip, total,
+    z_send, z_recv, t_send, t_recv, r_send, g_send, g_recv,
     x_send, x_recv, y_send, y_recv, c_send, c_recv, p_send, p_recv, s_send, s_recv,
-    load_sem, store_sem,
+    load_sem,
 ):
     half = act_ref.shape[0]
     rows, width = momentum.shape
     wide, middle, layers = width // 2, n // 2, n // 2
     core_rows, share = wide // 2, wide // groups
-    row_tile = half // 3 if half % 48 == 0 else half
+    pieces = 3 if half % 48 == 0 else 1
     a, b = lax.axis_index("aa"), lax.axis_index("ba")
     x, c, z, y = a // 2, a % 2, b // 2, b % 2
     core_mate = 2 * x + 1 - c
@@ -75,37 +74,54 @@
     sides = (z + layers - 1) // layers + (2 * layers - 2 - z) // layers
     pl.semaphore_wait(barrier, 2 * groups - 1 + sides)
 
-    def z_hop(source, layer, side):
-        return pltpu.make_async_remote_copy(
-            src_ref=source, dst_ref=line.at[layer],
-            send_sem=z_send.at[side, layer], recv_sem=z_recv.at[layer],
+    piece = half // pieces
+
+    def cut(j):
+        return pl.ds(j * piece, piece)
+
+    def z_hop(source, layer, side, j):
+        return pltpu.make_async_remote_copy(
+            src_ref=source.at[cut(j)], dst_ref=line.at[layer, cut(j)],
+            send_sem=z_send.at[side, layer, j], recv_sem=z_recv.at[layer, j],
             device_id={"ba": b + 2 - 4 * side}, device_id_type=MESH,
         )
 
-    def near_copy(source, layer):
-        return pltpu.make_async_remote_copy(
-            src_ref=source, dst_ref=tiles.at[y, a],
-            send_sem=t_send.at[0, layer], recv_sem=t_recv.at[y, a],
+    def near_copy(source, layer, j):
+        return pltpu.make_async_remote_copy(
+            src_ref=source.at[cut(j)], dst_ref=tiles.at[y, a, cut(j)],
+            send_sem=t_send.at[0, layer, j], recv_sem=t_recv.at[y, a, j],
             device_id={"aa": layer}, device_id_type=MESH,
         )
 
-    def far_copy(source, layer):
-        return pltpu.make_async_remote_copy(
-            src_ref=source, dst_ref=tiles.at[y, a],
-            send_sem=t_send.at[1, layer], recv_sem=t_recv.at[y, a],
+    def far_copy(source, layer, j):
+        return pltpu.make_async_remote_copy(
+            src_ref=source.at[cut(j)], dst_ref=tiles.at[y, a, cut(j)],
+            send_sem=t_send.at[1, layer, j], recv_sem=t_recv.at[y, a, j],
             device_id={"aa": layer, "ba": y_mate}, device_id_type=MESH,
         )
 
-    def deliver(source, layer):
-        far_copy(source, layer).start()
-
-        @pl.when(layer != a)
-        def _():
-            near_copy(source, layer).start()
+    def relay_copy(q, j):
+        origin = 2 * (1 - x) + q
+        return pltpu.make_async_remote_copy(
+            src_ref=tiles.at[y, origin, cut(j)], dst_ref=tiles.at[y, origin, cut(j)],
+            send_sem=r_send.at[q, j], recv_sem=t_recv.at[y, origin, j],
+            device_id={"ba": y_mate}, device_id_type=MESH,
+        )
+
+    def tile_arrival(k, r, j):
+        return pltpu.make_async_remote_copy(
+            src_ref=act_ref.at[cut(j)], dst_ref=tiles.at[k, r, cut(j)],
+            send_sem=t_send.at[0, 0, j], recv_sem=t_recv.at[k, r, j],
+            device_id={"aa": core_mate}, device_id_type=MESH,
+        )
+
+    def deliver(source, layer, j):
+        pl.when(layer // 2 == x)(far_copy(source, layer, j).start)
+        pl.when(layer != a)(near_copy(source, layer, j).start)
 
         @pl.when(layer == a)
         def _():
-            tiles[y, a] = source[...]
+            tiles[y, a, cut(j)] = source[cut(j)]
 
     def grad_copy(kind):
         mate = chip_mate if kind == 0 else core_mate
@@ -117,21 +133,32 @@
         )
 
     can_go = (z < layers - 1, z > 0)
-    for side in range(2):
-        pl.when(can_go[side])(z_hop(act_ref, z, side).start)
-    grad_copy(0).start()
-    grad_copy(1).start()
-    deliver(act_ref, z)
+    for j in range(pieces):
+        for side in range(2):
+            pl.when(can_go[side])(z_hop(act_ref, z, side, j).start)
+        deliver(act_ref, z, j)
+        if j == 0:
+            grad_copy(0).start()
+            grad_copy(1).start()
     grads[a] = grad_ref[...]
-    for distance in range(1, layers):
-        for side in range(2):
-            layer = z - distance if side == 0 else z + distance
-
-            @pl.when((layer >= 0) & (layer < layers))
-            def _():
-                z_hop(line.at[layer], layer, side).wait_recv()
-                pl.when(can_go[side])(z_hop(line.at[layer], layer, side).start)
-                deliver(line.at[layer], layer)
+    for distance in range(1, layers + 1):
+        if distance < layers:
+            for j in range(pieces):
+                for side in range(2):
+                    layer = z - distance if side == 0 else z + distance
+
+                    @pl.when((layer >= 0) & (layer < layers))
+                    def _():
+                        z_hop(line.at[layer], layer, side, j).wait_recv()
+                        pl.when(can_go[side])(z_hop(line.at[layer], layer, side, j).start)
+                        deliver(line.at[layer], layer, j)
+
+        @pl.when((z - a == distance - 1) | (a - z == distance - 1))
+        def _():
+            for j in range(pieces):
+                for q in range(2):
+                    tile_arrival(y, 2 * (1 - x) + q, j).wait_recv()
+                    relay_copy(q, j).start()
 
         if distance == 1:
             grad_copy(0).wait_recv()
@@ -141,7 +168,8 @@
     for load in loads:
         load.wait()
 
-    order = [(h, k) for k in range(2) for h in range(2)]
+    by_columns = [(h, k) for h in range(2) for k in range(2)]
+    by_halves = [(h, k) for k in range(2) for h in range(2)]
 
     def hop(held, send, recv, d, s, h, k):
         target = n - 1 if s == middle else 2 * s - 1 + d
@@ -153,35 +181,32 @@
             device_id={"ba": neighbours[d]}, device_id_type=MESH,
         )
 
-    def goes(by_rows, d, s, h, k):
-        return s < middle or d == (k if by_rows else h)
-
-    def pass_on(held, send, recv, by_rows, d, s, h, k):
+    def goes(first, d, s, h, k):
+        return s < middle or d == (k if first else h)
+
+    def pass_on(held, send, recv, first, d, s, h, k):
         hop(held, send, recv, d, s, h, k).wait_recv()
-        if s < middle and goes(by_rows, d, s + 1, h, k):
+        if s < middle and goes(first, d, s + 1, h, k):
             hop(held, send, recv, d, s + 1, h, k).start()
 
-    def drain(held, send, recv, by_rows):
+    def drain(held, send, recv, first):
         for s in range(1, middle + 1):
-            for h, k in order:
+            for h, k in by_columns:
                 for d in range(2):
-                    if goes(by_rows, d, s, h, k):
+                    if goes(first, d, s, h, k):
                         hop(held, send, recv, d, s, h, k).wait_send()
 
     for k in range(2):
         for r in range(groups):
-            pl.when((k != y) | (r != a))(
-                pltpu.make_async_remote_copy(
-                    src_ref=act_ref, dst_ref=tiles.at[k, r],
-                    send_sem=t_send.at[0, 0], recv_sem=t_recv.at[k, r],
-                    device_id={"aa": core_mate}, device_id_type=MESH,
-                ).wait_recv
-            )
-
-        @pl.loop(0, half // row_tile)
+            @pl.when((k != y) | ((r // 2 == x) & (r != a)))
+            def _():
+                for j in range(pieces):
+                    tile_arrival(k, r, j).wait_recv()
+
+        @pl.loop(0, pieces)
         def _(t):
-            source = pl.ds(pl.multiple_of(t * row_tile, 16), row_tile)
-            part = pl.ds(pl.multiple_of(k * half + t * row_tile, 16), row_tile)
+            source = pl.ds(pl.multiple_of(t * piece, 16), piece)
+            part = pl.ds(pl.multiple_of(k * half + t * piece, 16), piece)
             gradient = sum(
                 jnp.dot(tiles[k, r, source, :], grads[r], preferred_element_type=jnp.float32)
                 for r in range(groups)
@@ -192,12 +217,9 @@
             for h in range(2):
                 panel[0, h, part, :] = scaled[:, h * wide : (h + 1) * wide]
 
-        for h in range(2):
-            for d in range(2):
-                hop(panel, x_send, x_recv, d, 1, h, k).start()
-
-    store_momentum = pltpu.make_async_copy(momentum, new_momentum_hbm, store_sem.at[0])
-    store_momentum.start()
+    for h, k in by_columns:
+        for d in range(2):
+            hop(panel, x_send, x_recv, d, 1, h, k).start()
 
     def to_mate(source, target, send, recv, mate):
         return pltpu.make_async_remote_copy(
@@ -259,9 +281,9 @@
         share_copy(e, h, 2).wait_recv()
 
     def accumulate(held, e, halves, first, start, count):
-        @pl.loop(0, count // row_tile)
+        @pl.loop(0, count // half)
         def _(t):
-            part = pl.ds(pl.multiple_of(start + t * row_tile, 16), row_tile)
+            part = pl.ds(pl.multiple_of(start + t * half, 16), half)
             term = sum(
                 jnp.dot(
                     held[e, h, part, :], gram[e, h * wide : (h + 1) * wide, :],
@@ -274,55 +296,44 @@
             else:
                 total[part, :] += term
 
-    summed, shared = [], []
-
-    def advance():
-        for unit in shared:
-            relay(*unit)
-        for unit in summed:
-            gram_share(*unit)
-        shared[:] = summed
-        summed[:] = []
-
-    def use_units(units):
-        for unit in units:
-            gram_partial(*unit)
-        advance()
-        for unit in units:
-            core_sum(*unit)
-        summed[:] = units
-
     ring_x = (panel, x_send, x_recv, True)
-    use_units([(0, 0), (0, 1)])
-    for s in range(1, middle):
-        for i, (h, k) in enumerate(order):
-            for d in range(2):
-                pass_on(*ring_x, d, s, h, k)
-            if i == 1:
-                advance()
-        use_units([(e, h) for h in range(2) for e in (2 * s - 1, 2 * s)])
+    steps = [[(0, 0), (0, 1)]]
+    for unit in steps[0]:
+        gram_partial(*unit)
+    for s in range(1, middle + 1):
+        for h in range(2):
+            for k in range(2):
+                for d in range(2):
+                    if goes(True, d, s, h, k):
+                        pass_on(*ring_x, d, s, h, k)
+            if len(steps) == 1:
+                for unit in steps[0]:
+                    core_sum(*unit)
+            units = [(2 * s - 1, h), (2 * s, h)] if s < middle else [(n - 1, h)]
+            for unit in units:
+                gram_partial(*unit)
+            if len(steps) > 1:
+                for unit in steps[-2]:
+                    relay(*unit)
+            if (s, h) != (middle, 1):
+                for unit in steps[-1]:
+                    gram_share(*unit)
+                for unit in units:
+                    core_sum(*unit)
+            steps.append(units)
     last = n - 1
-    for h in range(2):
-        for d in range(2):
-            pass_on(*ring_x, d, middle, h, d)
-        if h == 0:
-            use_units([(last, 0)])
-    gram_partial(last, 1)
-    advance()
     for e in range(n):
         if e == 1:
             core_sum(last, 1)
-        if e == 3:
-            advance()
-            summed[:] = [(last, 1)]
+            gram_share(last, 0)
         if e == last - 2:
-            advance()
-        if e == last:
-            advance()
+            relay(last, 0)
+        if e == last - 1:
+            gram_share(last, 1)
         for h in range(2 if e < last else 1):
             gram_ready(e, h)
         accumulate(panel, e, (0, 1) if e < last else (0,), e == 0, 0, rows)
-    advance()
+    relay(last, 1)
     gram_ready(last, 1)
 
     ring_p = (powers, y_send, y_recv, False)
@@ -336,14 +347,13 @@
 
     accumulate(powers, 0, (0, 1), True, 0, rows)
     for s in range(1, middle):
-        for h, k in order:
+        for h, k in by_halves:
             for d in range(2):
                 pass_on(*ring_p, d, s, h, k)
         for e in (2 * s - 1, 2 * s):
             accumulate(powers, e, (0, 1), False, 0, rows)
 
     rate = step_ref[0] * factor
-    stores = []
     for k in range(2):
         for d in range(2):
             pass_on(*ring_p, d, middle, d, k)
@@ -357,12 +367,6 @@
                 + 2.0315 * total[part, columns]
             )
             weight[part, columns] = weight[part, columns] - rate * direction
-        stores.append(
-            pltpu.make_async_copy(
-                weight.at[part], new_weight_hbm.at[part], store_sem.at[1 + k]
-            )
-        )
-        stores[-1].start()
 
     drain(*ring_x)
     drain(*ring_p)
@@ -374,21 +378,22 @@
                 share_copy(e, h, step).wait_send()
     for kind in range(3):
         grad_copy(kind).wait_send()
-    for layer in range(layers):
-        far_copy(act_ref, layer).wait_send()
-        pl.when(layer != a)(near_copy(act_ref, layer).wait_send)
-        for side in range(2):
-            from_here = layer <= z if side == 0 else layer >= z
-            pl.when(from_here & can_go[side])(z_hop(act_ref, layer, side).wait_send)
-    store_momentum.wait()
-    for store in stores:
-        store.wait()
+    for j in range(pieces):
+        for q in range(2):
+            relay_copy(q, j).wait_send()
+        for layer in range(layers):
+            pl.when(layer // 2 == x)(far_copy(act_ref, layer, j).wait_send)
+            pl.when(layer != a)(near_copy(act_ref, layer, j).wait_send)
+            for side in range(2):
+                from_here = layer <= z if side == 0 else layer >= z
+                pl.when(from_here & can_go[side])(z_hop(act_ref, layer, side, j).wait_send)
 
 
 def fused_step(activations, out_grad, momentum, weight, norm_scale, step_size, n, groups):
     tokens, features = activations.shape
     rows, width = momentum.shape
     wide, middle = width // 2, n // 2
+    pieces = 3 if features % 48 == 0 else 1
     dma = pltpu.SemaphoreType.DMA
     vmem = pl.BlockSpec(memory_space=pltpu.VMEM)
     hbm = pl.BlockSpec(memory_space=pl.ANY)
@@ -402,7 +407,7 @@
             jax.ShapeDtypeStruct((rows, width), jnp.float32),
         ),
         in_specs=[vmem, vmem, hbm, hbm, smem, smem],
-        out_specs=(hbm, hbm),
+        out_specs=(vmem, vmem),
         scratch_shapes=[
             pltpu.VMEM((n // 2, features, tokens), jnp.bfloat16),
             pltpu.VMEM((2, groups, features, tokens), jnp.bfloat16),
@@ -414,18 +419,16 @@
             pltpu.VMEM((n, 2, wide // 2, width), jnp.float32),
             pltpu.VMEM((n, 2, wide // groups, width), jnp.float32),
             pltpu.VMEM((rows, width), jnp.float32),
-            pltpu.VMEM((rows, width), jnp.float32),
-            pltpu.VMEM((rows, width), jnp.float32),
-            dma((2, n // 2)), dma((n // 2,)),
-            dma((2, n // 2)), dma((2, groups)),
+            dma((2, n // 2, pieces)), dma((n // 2, pieces)),
+            dma((2, n // 2, pieces)), dma((2, groups, pieces)), dma((2, pieces)),
             dma((3,)), dma((3,)),
             ring, ring, ring, ring,
             units, units, units, units,
             dma((n, 2, 3)), dma((n, 2, 3)),
-            dma((2,)), dma((3,)),
+            dma((2,)),
         ],
         compiler_params=pltpu.CompilerParams(
-            collective_id=0, has_side_effects=True, vmem_limit_bytes=62 * 1024 * 1024
+            collective_id=0, has_side_effects=True, vmem_limit_bytes=48 * 1024 * 1024
         ),
         name="step",
     )(activations.T, out_grad, momentum, weight, norm_scale.reshape(1), step_size.reshape(1))

time: 252 us -> 233 us (0.925)
  Pallas kernels: 245 us -> 225 us
    pallas_call x1, Pallas kernels: 245 us -> 225 us  [fused_step(): pl.pallas_call(functools.partial(step_kernel, n, groups, 0.2 * math.sqrt(...]
where the time goes in v2:
time: 233 us; the launch traced here: 232 us
  Pallas kernels  225 us (97%)
  local copies, waits for them, and re-layouts  4.58 us (2%)
    pallas_call x1, Pallas kernels, fused_step(): pl.pallas_call(functools.partial(step_kernel, n, groups, 0.2 * math.sqrt(...  225 us

profile of v2, /device:TPU:0, one launch (start us, length us, event | category | flops | bytes accessed | tf_op | source)
XLA Modules:
  0.0 231.7 jit_solution(4548596216043045017)
XLA Ops:
  1.9 0.0 copy-start
  1.9 0.9 copy-done
  2.9 0.0 copy-start.1
  2.9 0.9 copy-done.1
  3.8 225.2 %step.1 = (f32[1056,512]{1,0:T(8,128)S(1)}, f32[1056,512]{1,0:T(8,128)S(1)}) custom-call(bf16[528,256]{1,0:T(8,128)(2,1)S(1)} %bitcast.5, bf16[256,512]{1,0:T(8,128)(2,1)S(1)} %copy-done.1, f32[1056,512]{1,0:T(8,128)} %momentum_hbm.1, f32[1056,512]{1,0:T(8,128)} %weight_hbm.1, f32[1]{0:T(128)} %bitcast.3.scale_ref, f32[1]{0:T(128)} %bitcast.4.step_ref), custom_call_target="tpu_custom_call" | custom-call | tf_op jit(solution)/shard_map/step/pallas_call | solution.py:403
  229.0 1.3 copy.12
  230.3 1.3 copy.13
Async XLA Ops:
  1.9 1.0 copy-start
  2.9 0.9 copy-start.1

commit v3 on v2

--- a/solution.py
+++ b/solution.py
@@ -21,14 +21,14 @@
 
 def step_kernel(
     n, groups, factor,
-    act_ref, grad_ref, momentum_hbm, weight_hbm, scale_ref, step_ref,
+    act_hbm, grad_hbm, momentum_hbm, weight_hbm, scale_ref, step_ref,
     weight, momentum,
-    line, tiles, grads, panel, powers, gram, parts, from_core, from_chip, total,
-    z_send, z_recv, t_send, t_recv, r_send, g_send, g_recv,
+    line, stage, tiles, grads, panel, powers, gram, parts, from_core, from_chip, total,
+    z_send, z_recv, t_send, t_recv, b_recv, g_send, g_recv,
     x_send, x_recv, y_send, y_recv, c_send, c_recv, p_send, p_recv, s_send, s_recv,
     load_sem,
 ):
-    half = act_ref.shape[0]
+    half = line.shape[1]
     rows, width = momentum.shape
     wide, middle, layers = width // 2, n // 2, n // 2
     core_rows, share = wide // 2, wide // groups
@@ -40,8 +40,10 @@
     y_mate = 2 * z + 1 - y
 
     loads = [
-        pltpu.make_async_copy(momentum_hbm, momentum, load_sem.at[0]),
-        pltpu.make_async_copy(weight_hbm, weight, load_sem.at[1]),
+        pltpu.make_async_copy(act_hbm, line.at[z], load_sem.at[0]),
+        pltpu.make_async_copy(grad_hbm, grads.at[a], load_sem.at[1]),
+        pltpu.make_async_copy(momentum_hbm, momentum, load_sem.at[2]),
+        pltpu.make_async_copy(weight_hbm, weight, load_sem.at[3]),
     ]
     for load in loads:
         load.start()
@@ -79,68 +81,76 @@
     def cut(j):
         return pl.ds(j * piece, piece)
 
-    def z_hop(source, layer, side, j):
+    def remote(source, target, send, recv, where):
         return pltpu.make_async_remote_copy(
-            src_ref=source.at[cut(j)], dst_ref=line.at[layer, cut(j)],
-            send_sem=z_send.at[side, layer, j], recv_sem=z_recv.at[layer, j],
-            device_id={"ba": b + 2 - 4 * side}, device_id_type=MESH,
-        )
-
-    def near_copy(source, layer, j):
-        return pltpu.make_async_remote_copy(
-            src_ref=source.at[cut(j)], dst_ref=tiles.at[y, a, cut(j)],
-            send_sem=t_send.at[0, layer, j], recv_sem=t_recv.at[y, a, j],
-            device_id={"aa": layer}, device_id_type=MESH,
-        )
-
-    def far_copy(source, layer, j):
-        return pltpu.make_async_remote_copy(
-            src_ref=source.at[cut(j)], dst_ref=tiles.at[y, a, cut(j)],
-            send_sem=t_send.at[1, layer, j], recv_sem=t_recv.at[y, a, j],
-            device_id={"aa": layer, "ba": y_mate}, device_id_type=MESH,
-        )
-
-    def relay_copy(q, j):
-        origin = 2 * (1 - x) + q
-        return pltpu.make_async_remote_copy(
-            src_ref=tiles.at[y, origin, cut(j)], dst_ref=tiles.at[y, origin, cut(j)],
-            send_sem=r_send.at[q, j], recv_sem=t_recv.at[y, origin, j],
-            device_id={"ba": y_mate}, device_id_type=MESH,
+            src_ref=source, dst_ref=target, send_sem=send, recv_sem=recv,
+            device_id=where, device_id_type=MESH,
+        )
+
+    def z_hop(layer, side, j):
+        block = line.at[layer, cut(j)]
+        return remote(
+            block, block, z_send.at[side, layer], z_recv.at[layer, j], {"ba": b + 2 - 4 * side}
+        )
+
+    def near_copy(layer, j):
+        return remote(
+            line.at[layer, cut(j)], tiles.at[y, a, cut(j)], t_send.at[0], t_recv.at[y, a, j],
+            {"aa": layer},
+        )
+
+    def far_copy(layer, j):
+        return remote(
+            line.at[layer, cut(j)], tiles.at[y, a, cut(j)], t_send.at[1], t_recv.at[y, a, j],
+            {"aa": layer, "ba": y_mate},
+        )
+
+    def relay_copy(j):
+        block = tiles.at[y, 2 * (1 - x), cut(j)]
+        return remote(block, block, t_send.at[2], t_recv.at[y, 2 * (1 - x), j], {"ba": y_mate})
+
+    def side_copy(layer, j):
+        return remote(
+            line.at[layer, cut(j)], stage.at[layer % 2, cut(j)], t_send.at[3],
+            b_recv.at[layer % 2, j], {"ba": y_mate},
+        )
+
+    def cross_copy(slot, j):
+        return remote(
+            stage.at[slot, cut(j)], tiles.at[1 - y, a, cut(j)], t_send.at[4],
+            t_recv.at[1 - y, a, j], {"aa": 2 * (1 - x) + slot},
         )
 
     def tile_arrival(k, r, j):
-        return pltpu.make_async_remote_copy(
-            src_ref=act_ref.at[cut(j)], dst_ref=tiles.at[k, r, cut(j)],
-            send_sem=t_send.at[0, 0, j], recv_sem=t_recv.at[k, r, j],
-            device_id={"aa": core_mate}, device_id_type=MESH,
-        )
-
-    def deliver(source, layer, j):
-        pl.when(layer // 2 == x)(far_copy(source, layer, j).start)
-        pl.when(layer != a)(near_copy(source, layer, j).start)
+        block = tiles.at[k, r, cut(j)]
+        return remote(block, block, t_send.at[0], t_recv.at[k, r, j], {"aa": core_mate})
+
+    def deliver(layer, j):
+        pl.when(layer // 2 == x)(far_copy(layer, j).start)
+        pl.when((layer // 2 != x) & (c == 1))(side_copy(layer, j).start)
+        pl.when(layer != a)(near_copy(layer, j).start)
 
         @pl.when(layer == a)
         def _():
-            tiles[y, a, cut(j)] = source[cut(j)]
+            tiles[y, a, cut(j)] = line[layer, cut(j)]
 
     def grad_copy(kind):
-        mate = chip_mate if kind == 0 else core_mate
-        source, slot = (grads.at[chip_mate], chip_mate) if kind == 2 else (grad_ref, a)
-        return pltpu.make_async_remote_copy(
-            src_ref=source, dst_ref=grads.at[slot],
-            send_sem=g_send.at[kind], recv_sem=g_recv.at[kind],
-            device_id={"aa": mate}, device_id_type=MESH,
-        )
-
+        slot = chip_mate if kind == 2 else a
+        return remote(
+            grads.at[slot], grads.at[slot], g_send.at[kind], g_recv.at[kind],
+            {"aa": chip_mate if kind == 0 else core_mate},
+        )
+
+    loads[0].wait()
+    loads[1].wait()
     can_go = (z < layers - 1, z > 0)
     for j in range(pieces):
         for side in range(2):
-            pl.when(can_go[side])(z_hop(act_ref, z, side, j).start)
-        deliver(act_ref, z, j)
+            pl.when(can_go[side])(z_hop(z, side, j).start)
+        deliver(z, j)
         if j == 0:
             grad_copy(0).start()
             grad_copy(1).start()
-    grads[a] = grad_ref[...]
     for distance in range(1, layers + 1):
         if distance < layers:
             for j in range(pieces):
@@ -149,24 +159,33 @@
 
                     @pl.when((layer >= 0) & (layer < layers))
                     def _():
-                        z_hop(line.at[layer], layer, side, j).wait_recv()
-                        pl.when(can_go[side])(z_hop(line.at[layer], layer, side, j).start)
-                        deliver(line.at[layer], layer, j)
+                        z_hop(layer, side, j).wait_recv()
+                        pl.when(can_go[side])(z_hop(layer, side, j).start)
+                        deliver(layer, j)
+
+        for side in range(2):
+            layer = z - distance + 1 if side == 0 else z + distance - 1
+            there = (layer >= 0) & (layer < layers) & ((side == 0) | (distance > 1))
+
+            @pl.when(there & (layer // 2 != x) & (c == 1))
+            def _():
+                for j in range(pieces):
+                    side_copy(layer, j).wait_recv()
+                    cross_copy(layer % 2, j).start()
 
         @pl.when((z - a == distance - 1) | (a - z == distance - 1))
         def _():
             for j in range(pieces):
-                for q in range(2):
-                    tile_arrival(y, 2 * (1 - x) + q, j).wait_recv()
-                    relay_copy(q, j).start()
+                tile_arrival(y, 2 * (1 - x), j).wait_recv()
+                relay_copy(j).start()
 
         if distance == 1:
             grad_copy(0).wait_recv()
             grad_copy(2).start()
     grad_copy(1).wait_recv()
     grad_copy(2).wait_recv()
-    for load in loads:
-        load.wait()
+    loads[2].wait()
+    loads[3].wait()
 
     by_columns = [(h, k) for h in range(2) for k in range(2)]
     by_halves = [(h, k) for k in range(2) for h in range(2)]
@@ -177,7 +196,7 @@
         part = pl.ds(k * half, half)
         return pltpu.make_async_remote_copy(
             src_ref=held.at[origin, h, part], dst_ref=held.at[target, h, part],
-            send_sem=send.at[d, s - 1, h, k], recv_sem=recv.at[d, s - 1, h, k],
+            send_sem=send, recv_sem=recv.at[d, s - 1, h, k],
             device_id={"ba": neighbours[d]}, device_id_type=MESH,
         )
 
@@ -189,16 +208,9 @@
         if s < middle and goes(first, d, s + 1, h, k):
             hop(held, send, recv, d, s + 1, h, k).start()
 
-    def drain(held, send, recv, first):
-        for s in range(1, middle + 1):
-            for h, k in by_columns:
-                for d in range(2):
-                    if goes(first, d, s, h, k):
-                        hop(held, send, recv, d, s, h, k).wait_send()
-
     for k in range(2):
         for r in range(groups):
-            @pl.when((k != y) | ((r // 2 == x) & (r != a)))
+            @pl.when((k != y) | ((r != 2 * (1 - x)) & (r != a)))
             def _():
                 for j in range(pieces):
                     tile_arrival(k, r, j).wait_recv()
@@ -213,7 +225,7 @@
             )
             updated = 0.95 * momentum[part, :] + gradient
             momentum[part, :] = updated
-            scaled = (updated / scale_ref[0]).astype(jnp.bfloat16)
+            scaled = (updated / scale_ref[()]).astype(jnp.bfloat16)
             for h in range(2):
                 panel[0, h, part, :] = scaled[:, h * wide : (h + 1) * wide]
 
@@ -221,34 +233,28 @@
         for d in range(2):
             hop(panel, x_send, x_recv, d, 1, h, k).start()
 
-    def to_mate(source, target, send, recv, mate):
-        return pltpu.make_async_remote_copy(
-            src_ref=source, dst_ref=target, send_sem=send, recv_sem=recv,
-            device_id={"aa": mate}, device_id_type=MESH,
-        )
-
     def span(start, size):
         return pl.ds(pl.multiple_of(start, size), size)
 
     mine, theirs = c * core_rows + x * share, c * core_rows + (1 - x) * share
 
     def core_copy(e, h):
-        return to_mate(
+        return remote(
             parts.at[e, h, span((1 - c) * core_rows, core_rows)], from_core.at[e, h],
-            c_send.at[e, h], c_recv.at[e, h], core_mate,
+            c_send, c_recv.at[e, h], {"aa": core_mate},
         )
 
     def chip_copy(e, h):
-        return to_mate(
+        return remote(
             parts.at[e, h, span(theirs, share)], from_chip.at[e, h],
-            p_send.at[e, h], p_recv.at[e, h], chip_mate,
+            p_send, p_recv.at[e, h], {"aa": chip_mate},
         )
 
     def share_copy(e, h, step):
-        rows_of = gram.at[e, span(h * wide + (theirs if step == 2 else mine), share)]
-        return to_mate(
-            rows_of, rows_of, s_send.at[e, h, step], s_recv.at[e, h, step],
-            chip_mate if step == 0 else core_mate,
+        block = gram.at[e, span(h * wide + (theirs if step == 2 else mine), share)]
+        return remote(
+            block, block, s_send.at[step], s_recv.at[e, h, min(step, 1)],
+            {"aa": chip_mate if step == 0 else core_mate},
         )
 
     def gram_partial(e, h):
@@ -277,8 +283,10 @@
         share_copy(e, h, 2).start()
 
     def gram_ready(e, h):
-        share_copy(e, h, 1).wait_recv()
-        share_copy(e, h, 2).wait_recv()
+        block = gram.at[e, span(h * wide + (1 - c) * core_rows, core_rows)]
+        remote(
+            block, block, s_send.at[1], s_recv.at[e, h, 1], {"aa": core_mate}
+        ).wait_recv()
 
     def accumulate(held, e, halves, first, start, count):
         @pl.loop(0, count // half)
@@ -297,39 +305,50 @@
                 total[part, :] += term
 
     ring_x = (panel, x_send, x_recv, True)
-    steps = [[(0, 0), (0, 1)]]
+    last = n - 1
+    steps = [[(0, h) for h in range(2)]]
+    for s in range(1, middle + 1):
+        for h in range(2):
+            steps.append([(2 * s - 1, h), (2 * s, h)] if s < middle else [(last, h)])
+    final = len(steps) - 1
     for unit in steps[0]:
         gram_partial(*unit)
-    for s in range(1, middle + 1):
-        for h in range(2):
-            for k in range(2):
-                for d in range(2):
-                    if goes(True, d, s, h, k):
-                        pass_on(*ring_x, d, s, h, k)
-            if len(steps) == 1:
-                for unit in steps[0]:
-                    core_sum(*unit)
-            units = [(2 * s - 1, h), (2 * s, h)] if s < middle else [(n - 1, h)]
-            for unit in units:
-                gram_partial(*unit)
-            if len(steps) > 1:
-                for unit in steps[-2]:
-                    relay(*unit)
-            if (s, h) != (middle, 1):
-                for unit in steps[-1]:
-                    gram_share(*unit)
-                for unit in units:
-                    core_sum(*unit)
-            steps.append(units)
-    last = n - 1
+    for i in range(1, final + 1):
+        s, h = (i + 1) // 2, (i + 1) % 2
+        for k in range(2):
+            for d in range(2):
+                if goes(True, d, s, h, k):
+                    pass_on(*ring_x, d, s, h, k)
+        if i == 1:
+            for unit in steps[0]:
+                core_sum(*unit)
+        for unit in steps[i]:
+            gram_partial(*unit)
+        if i >= 4:
+            for unit in steps[i - 3]:
+                relay(*unit)
+        if i >= 3:
+            for unit in steps[i - 2]:
+                gram_share(*unit)
+        if i == 3:
+            for unit in steps[0]:
+                relay(*unit)
+        if i == 2:
+            for unit in steps[0]:
+                gram_share(*unit)
+        if i < final:
+            for unit in steps[i]:
+                core_sum(*unit)
+    chores = {
+        1: [(core_sum, final)],
+        2: [(relay, final - 2)],
+        3: [(gram_share, final - 1)],
+        6: [(gram_share, final), (relay, final - 1)],
+    }
     for e in range(n):
-        if e == 1:
-            core_sum(last, 1)
-            gram_share(last, 0)
-        if e == last - 2:
-            relay(last, 0)
-        if e == last - 1:
-            gram_share(last, 1)
+        for do, i in chores.get(e, []):
+            for unit in steps[i]:
+                do(*unit)
         for h in range(2 if e < last else 1):
             gram_ready(e, h)
         accumulate(panel, e, (0, 1) if e < last else (0,), e == 0, 0, rows)
@@ -353,7 +372,7 @@
         for e in (2 * s - 1, 2 * s):
             accumulate(powers, e, (0, 1), False, 0, rows)
 
-    rate = step_ref[0] * factor
+    rate = step_ref[()] * factor
     for k in range(2):
         for d in range(2):
             pass_on(*ring_p, d, middle, d, k)
@@ -368,25 +387,33 @@
             )
             weight[part, columns] = weight[part, columns] - rate * direction
 
-    drain(*ring_x)
-    drain(*ring_p)
-    for e in range(n):
-        for h in range(2):
-            core_copy(e, h).wait_send()
-            chip_copy(e, h).wait_send()
-            for step in range(3):
-                share_copy(e, h, step).wait_send()
+    def sent(block, send):
+        remote(block, block, send, x_recv.at[0, 0, 0, 0], {"aa": core_mate}).wait_send()
+
+    sent(panel.at[pl.ds(1, n - 1)], x_send)
+    sent(powers.at[pl.ds(1, n - 1)], y_send)
+    sent(from_core, c_send)
+    sent(from_chip, p_send)
+    for step in range(3):
+        sent(gram.at[pl.ds(0, n // groups)], s_send.at[step])
     for kind in range(3):
         grad_copy(kind).wait_send()
-    for j in range(pieces):
-        for q in range(2):
-            relay_copy(q, j).wait_send()
-        for layer in range(layers):
-            pl.when(layer // 2 == x)(far_copy(act_ref, layer, j).wait_send)
-            pl.when(layer != a)(near_copy(act_ref, layer, j).wait_send)
-            for side in range(2):
-                from_here = layer <= z if side == 0 else layer >= z
-                pl.when(from_here & can_go[side])(z_hop(act_ref, layer, side, j).wait_send)
+    sent(line.at[pl.ds(0, layers - 1)], t_send.at[0])
+    sent(line.at[pl.ds(0, 2)], t_send.at[1])
+    sent(line.at[0], t_send.at[2])
+
+    @pl.when(c == 1)
+    def _():
+        sent(line.at[pl.ds(0, 2)], t_send.at[3])
+        sent(line.at[pl.ds(0, 2)], t_send.at[4])
+
+    for layer in range(layers):
+        for side in range(2):
+            from_here = layer <= z if side == 0 else layer >= z
+
+            @pl.when(from_here & can_go[side])
+            def _():
+                sent(line.at[layer], z_send.at[side, layer])
 
 
 def fused_step(activations, out_grad, momentum, weight, norm_scale, step_size, n, groups):
@@ -396,7 +423,7 @@
     pieces = 3 if features % 48 == 0 else 1
     dma = pltpu.SemaphoreType.DMA
     vmem = pl.BlockSpec(memory_space=pltpu.VMEM)
-    hbm = pl.BlockSpec(memory_space=pl.ANY)
+    hbm = pl.BlockSpec(memory_space=pltpu.HBM)
     smem = pl.BlockSpec(memory_space=pltpu.SMEM)
     ring = dma((2, middle, 2, 2))
     units = dma((n, 2))
@@ -406,10 +433,11 @@
             jax.ShapeDtypeStruct((rows, width), jnp.float32),
             jax.ShapeDtypeStruct((rows, width), jnp.float32),
         ),
-        in_specs=[vmem, vmem, hbm, hbm, smem, smem],
+        in_specs=[hbm, hbm, hbm, hbm, smem, smem],
         out_specs=(vmem, vmem),
         scratch_shapes=[
             pltpu.VMEM((n // 2, features, tokens), jnp.bfloat16),
+            pltpu.VMEM((2, features, tokens), jnp.bfloat16),
             pltpu.VMEM((2, groups, features, tokens), jnp.bfloat16),
             pltpu.VMEM((groups, tokens, width), jnp.bfloat16),
             pltpu.VMEM((n, 2, rows, wide), jnp.bfloat16),
@@ -419,19 +447,21 @@
             pltpu.VMEM((n, 2, wide // 2, width), jnp.float32),
             pltpu.VMEM((n, 2, wide // groups, width), jnp.float32),
             pltpu.VMEM((rows, width), jnp.float32),
-            dma((2, n // 2, pieces)), dma((n // 2, pieces)),
-            dma((2, n // 2, pieces)), dma((2, groups, pieces)), dma((2, pieces)),
+            dma((2, n // 2)), dma((n // 2, pieces)),
+            dma((5,)), dma((2, groups, pieces)), dma((2, pieces)),
             dma((3,)), dma((3,)),
-            ring, ring, ring, ring,
-            units, units, units, units,
-            dma((n, 2, 3)), dma((n, 2, 3)),
-            dma((2,)),
+            dma, ring, dma, ring,
+            dma, units, dma, units,
+            dma((3,)), dma((n, 2, 2)),
+            dma((4,)),
         ],
         compiler_params=pltpu.CompilerParams(
             collective_id=0, has_side_effects=True, vmem_limit_bytes=48 * 1024 * 1024
         ),
         name="step",
-    )(activations.T, out_grad, momentum, weight, norm_scale.reshape(1), step_size.reshape(1))
+    )(
+        pltpu.with_memory_space_constraint(activations.T, pltpu.HBM),
+        pltpu.with_memory_space_constraint(out_grad, pltpu.HBM), momentum, weight, norm_scale, step_size)
 
 
 def plain_gradient(activations, out_grad):

time: 233 us -> 228 us (0.979)
  Pallas kernels: 225 us -> 220 us
    pallas_call x1, Pallas kernels: 225 us -> 220 us  [fused_step(): pl.pallas_call(functools.partial(step_kernel, n, groups, 0.2 * math.sqrt(...]
where the time goes in v3:
time: 228 us; the launch traced here: 225 us
  Pallas kernels  220 us (96%)
  local copies, waits for them, and re-layouts  2.68 us (1%)
    pallas_call x1, Pallas kernels, fused_step(): pl.pallas_call(functools.partial(step_kernel, n, groups, 0.2 * math.sqrt(...  220 us

profile of v3, /device:TPU:0, one launch (start us, length us, event | category | flops | bytes accessed | tf_op | source)
XLA Modules:
  0.0 224.6 jit_solution(18076086043088178771)
XLA Ops:
  1.9 220.0 %step.1 = (f32[1056,512]{1,0:T(8,128)S(1)}, f32[1056,512]{1,0:T(8,128)S(1)}) custom-call(bf16[528,256]{1,0:T(8,128)(2,1)} %bitcast.1, bf16[256,512]{1,0:T(8,128)(2,1)} %grad_hbm.1, f32[1056,512]{1,0:T(8,128)} %momentum_hbm.1, f32[1056,512]{1,0:T(8,128)} %weight_hbm.1, f32[]{:T(128)S(6)} %copy.10.scale_ref, f32[]{:T(128)S(6)} %copy.11.step_ref), custom_call_target="tpu_custom_call" | custom-call | tf_op jit(solution)/shard_map/step/pallas_call | solution.py:430
  221.9 1.3 copy.12
  223.3 1.3 copy.13

commit v4 on v3

--- a/solution.py
+++ b/solution.py
@@ -190,37 +190,43 @@
     by_columns = [(h, k) for h in range(2) for k in range(2)]
     by_halves = [(h, k) for k in range(2) for h in range(2)]
 
-    def hop(held, send, recv, d, s, h, k):
+    def row_half(position, k):
+        position = (position + n) % n
+        return pl.ds(pl.multiple_of((position // middle + k) % 2 * half, 16), half)
+
+    def hop(held, send, recv, first, d, s, h, k, arrival=False):
         target = n - 1 if s == middle else 2 * s - 1 + d
         origin = 0 if s == 1 else 2 * s - 3 + d
-        part = pl.ds(k * half, half)
-        return pltpu.make_async_remote_copy(
-            src_ref=held.at[origin, h, part], dst_ref=held.at[target, h, part],
-            send_sem=send, recv_sem=recv.at[d, s - 1, h, k],
-            device_id={"ba": neighbours[d]}, device_id_type=MESH,
+        steps_back = s if arrival else s - 1
+        part = row_half(place - steps_back + 2 * d * steps_back, k) if first else pl.ds(k * half, half)
+        return remote(
+            held.at[origin, h, part], held.at[target, h, part], send, recv.at[d, s - 1, h, k],
+            {"ba": neighbours[d]},
         )
 
     def goes(first, d, s, h, k):
         return s < middle or d == (k if first else h)
 
     def pass_on(held, send, recv, first, d, s, h, k):
-        hop(held, send, recv, d, s, h, k).wait_recv()
+        hop(held, send, recv, first, d, s, h, k, arrival=True).wait_recv()
         if s < middle and goes(first, d, s + 1, h, k):
-            hop(held, send, recv, d, s + 1, h, k).start()
-
+            hop(held, send, recv, first, d, s + 1, h, k).start()
+
+    ring_x = (panel, x_send, x_recv, True)
     for k in range(2):
+        owner = y if k == 0 else 1 - y
         for r in range(groups):
-            @pl.when((k != y) | ((r != 2 * (1 - x)) & (r != a)))
+            @pl.when((r != 2 * (1 - x)) & (r != a) if k == 0 else r >= 0)
             def _():
                 for j in range(pieces):
-                    tile_arrival(k, r, j).wait_recv()
+                    tile_arrival(owner, r, j).wait_recv()
 
         @pl.loop(0, pieces)
         def _(t):
             source = pl.ds(pl.multiple_of(t * piece, 16), piece)
-            part = pl.ds(pl.multiple_of(k * half + t * piece, 16), piece)
+            part = pl.ds(pl.multiple_of(owner * half + t * piece, 16), piece)
             gradient = sum(
-                jnp.dot(tiles[k, r, source, :], grads[r], preferred_element_type=jnp.float32)
+                jnp.dot(tiles[owner, r, source, :], grads[r], preferred_element_type=jnp.float32)
                 for r in range(groups)
             )
             updated = 0.95 * momentum[part, :] + gradient
@@ -229,9 +235,13 @@
             for h in range(2):
                 panel[0, h, part, :] = scaled[:, h * wide : (h + 1) * wide]
 
-    for h, k in by_columns:
+        if k == 0:
+            for d in range(2):
+                hop(*ring_x, d, 1, 0, 0).start()
+
+    for h, k in by_columns[1:]:
         for d in range(2):
-            hop(panel, x_send, x_recv, d, 1, h, k).start()
+            hop(*ring_x, d, 1, h, k).start()
 
     def span(start, size):
         return pl.ds(pl.multiple_of(start, size), size)
@@ -304,51 +314,45 @@
             else:
                 total[part, :] += term
 
-    ring_x = (panel, x_send, x_recv, True)
     last = n - 1
     steps = [[(0, h) for h in range(2)]]
     for s in range(1, middle + 1):
         for h in range(2):
             steps.append([(2 * s - 1, h), (2 * s, h)] if s < middle else [(last, h)])
     final = len(steps) - 1
-    for unit in steps[0]:
-        gram_partial(*unit)
+
+    def each(do, i):
+        for unit in steps[i]:
+            do(*unit)
+
+    each(gram_partial, 0)
     for i in range(1, final + 1):
         s, h = (i + 1) // 2, (i + 1) % 2
         for k in range(2):
             for d in range(2):
                 if goes(True, d, s, h, k):
                     pass_on(*ring_x, d, s, h, k)
+            if k == 0 and 1 < i < final - 1:
+                each(gram_share, i - 1)
         if i == 1:
-            for unit in steps[0]:
-                core_sum(*unit)
-        for unit in steps[i]:
-            gram_partial(*unit)
-        if i >= 4:
-            for unit in steps[i - 3]:
-                relay(*unit)
-        if i >= 3:
-            for unit in steps[i - 2]:
-                gram_share(*unit)
+            each(core_sum, 0)
+        each(gram_partial, i)
+        if i == 2:
+            each(gram_share, 0)
+        each(core_sum, i)
         if i == 3:
-            for unit in steps[0]:
-                relay(*unit)
-        if i == 2:
-            for unit in steps[0]:
-                gram_share(*unit)
-        if i < final:
-            for unit in steps[i]:
-                core_sum(*unit)
-    chores = {
-        1: [(core_sum, final)],
-        2: [(relay, final - 2)],
-        3: [(gram_share, final - 1)],
-        6: [(gram_share, final), (relay, final - 1)],
-    }
+            each(relay, 0)
+        if 1 < i < final - 1:
+            each(relay, i - 1)
+        if i == final - 1:
+            each(gram_share, i - 1)
+    each(relay, final - 2)
+    each(gram_share, final - 1)
     for e in range(n):
-        for do, i in chores.get(e, []):
-            for unit in steps[i]:
-                do(*unit)
+        if e == 4:
+            each(gram_share, final)
+        if e == 5:
+            each(relay, final - 1)
         for h in range(2 if e < last else 1):
             gram_ready(e, h)
         accumulate(panel, e, (0, 1) if e < last else (0,), e == 0, 0, rows)
@@ -362,7 +366,7 @@
         for h in range(2):
             powers[0, h, part, :] = total[part, h * wide : (h + 1) * wide].astype(jnp.bfloat16)
             for d in range(2):
-                hop(powers, y_send, y_recv, d, 1, h, k).start()
+                hop(*ring_p, d, 1, h, k).start()
 
     accumulate(powers, 0, (0, 1), True, 0, rows)
     for s in range(1, middle):

time: 228 us -> 219 us (0.961)
  Pallas kernels: 220 us -> 213 us
    pallas_call x1, Pallas kernels: 220 us -> 213 us  [fused_step(): pl.pallas_call(functools.partial(step_kernel, n, groups, 0.2 * math.sqrt(...]
where the time goes in v4:
time: 219 us; the launch traced here: 217 us
  Pallas kernels  213 us (97%)
  local copies, waits for them, and re-layouts  2.68 us (1%)
    pallas_call x1, Pallas kernels, fused_step(): pl.pallas_call(functools.partial(step_kernel, n, groups, 0.2 * math.sqrt(...  213 us

profile of v4, /device:TPU:0, one launch (start us, length us, event | category | flops | bytes accessed | tf_op | source)
XLA Modules:
  0.0 217.4 jit_solution(7921227881064306366)
XLA Ops:
  1.9 212.7 %step.1 = (f32[1056,512]{1,0:T(8,128)S(1)}, f32[1056,512]{1,0:T(8,128)S(1)}) custom-call(bf16[528,256]{1,0:T(8,128)(2,1)} %bitcast.1, bf16[256,512]{1,0:T(8,128)(2,1)} %grad_hbm.1, f32[1056,512]{1,0:T(8,128)} %momentum_hbm.1, f32[1056,512]{1,0:T(8,128)} %weight_hbm.1, f32[]{:T(128)S(6)} %copy.10.scale_ref, f32[]{:T(128)S(6)} %copy.11.step_ref), custom_call_target="tpu_custom_call" | custom-call | tf_op jit(solution)/shard_map/step/pallas_call | solution.py:434
  214.7 1.3 copy.12
  216.0 1.3 copy.13

commit v5 on v4

--- a/solution.py
+++ b/solution.py
@@ -31,7 +31,7 @@
     half = line.shape[1]
     rows, width = momentum.shape
     wide, middle, layers = width // 2, n // 2, n // 2
-    core_rows, share = wide // 2, wide // groups
+    narrow = wide // 2
     pieces = 3 if half % 48 == 0 else 1
     a, b = lax.axis_index("aa"), lax.axis_index("ba")
     x, c, z, y = a // 2, a % 2, b // 2, b % 2
@@ -187,32 +187,50 @@
     loads[2].wait()
     loads[3].wait()
 
-    by_columns = [(h, k) for h in range(2) for k in range(2)]
-    by_halves = [(h, k) for k in range(2) for h in range(2)]
-
     def row_half(position, k):
         position = (position + n) % n
         return pl.ds(pl.multiple_of((position // middle + k) % 2 * half, 16), half)
 
-    def hop(held, send, recv, first, d, s, h, k, arrival=False):
+    def hop_x(d, s, p, arrival=False):
         target = n - 1 if s == middle else 2 * s - 1 + d
         origin = 0 if s == 1 else 2 * s - 3 + d
-        steps_back = s if arrival else s - 1
-        part = row_half(place - steps_back + 2 * d * steps_back, k) if first else pl.ds(k * half, half)
-        return remote(
-            held.at[origin, h, part], held.at[target, h, part], send, recv.at[d, s - 1, h, k],
-            {"ba": neighbours[d]},
-        )
-
-    def goes(first, d, s, h, k):
-        return s < middle or d == (k if first else h)
-
-    def pass_on(held, send, recv, first, d, s, h, k):
-        hop(held, send, recv, first, d, s, h, k, arrival=True).wait_recv()
-        if s < middle and goes(first, d, s + 1, h, k):
-            hop(held, send, recv, first, d, s + 1, h, k).start()
-
-    ring_x = (panel, x_send, x_recv, True)
+        if p < 2:
+            back = s if arrival else s - 1
+            cut_out = (0, row_half(place - back + 2 * d * back, p))
+        else:
+            cut_out = (
+                1, pl.ds(d * half, half) if s == middle else pl.ds(0, rows),
+                pl.ds((p - 2) * narrow, narrow),
+            )
+        return remote(
+            panel.at[(origin, *cut_out)], panel.at[(target, *cut_out)],
+            x_send, x_recv.at[d, s - 1, p], {"ba": neighbours[d]},
+        )
+
+    def goes_x(d, s, p):
+        return s < middle or p > 1 or d == p
+
+    def pass_x(s, p):
+        for d in range(2):
+            if goes_x(d, s, p):
+                hop_x(d, s, p, arrival=True).wait_recv()
+                if s < middle and goes_x(d, s + 1, p):
+                    hop_x(d, s + 1, p).start()
+
+    def hop_p(d, s, h, k):
+        target = n - 1 if s == middle else 2 * s - 1 + d
+        origin = 0 if s == 1 else 2 * s - 3 + d
+        part = pl.ds(k * half, half)
+        return remote(
+            powers.at[origin, h, part], powers.at[target, h, part],
+            y_send, y_recv.at[d, s - 1, h, k], {"ba": neighbours[d]},
+        )
+
+    def pass_p(d, s, h, k):
+        hop_p(d, s, h, k).wait_recv()
+        if s + 1 < middle or (s + 1 == middle and d == h):
+            hop_p(d, s + 1, h, k).start()
+
     for k in range(2):
         owner = y if k == 0 else 1 - y
         for r in range(groups):
@@ -237,65 +255,84 @@
 
         if k == 0:
             for d in range(2):
-                hop(*ring_x, d, 1, 0, 0).start()
-
-    for h, k in by_columns[1:]:
+                hop_x(d, 1, 0).start()
+
+    for p in range(1, 4):
         for d in range(2):
-            hop(*ring_x, d, 1, h, k).start()
+            hop_x(d, 1, p).start()
 
     def span(start, size):
-        return pl.ds(pl.multiple_of(start, size), size)
-
-    mine, theirs = c * core_rows + x * share, c * core_rows + (1 - x) * share
-
-    def core_copy(e, h):
-        return remote(
-            parts.at[e, h, span((1 - c) * core_rows, core_rows)], from_core.at[e, h],
-            c_send, c_recv.at[e, h], {"aa": core_mate},
-        )
-
-    def chip_copy(e, h):
-        return remote(
-            parts.at[e, h, span(theirs, share)], from_chip.at[e, h],
-            p_send, p_recv.at[e, h], {"aa": chip_mate},
-        )
-
-    def share_copy(e, h, step):
-        block = gram.at[e, span(h * wide + (theirs if step == 2 else mine), share)]
-        return remote(
-            block, block, s_send.at[step], s_recv.at[e, h, min(step, 1)],
+        return pl.ds(pl.multiple_of(start, 16), size)
+
+    sizes, starts = (wide, narrow, narrow), (0, wide, wide + narrow)
+
+    def rows_of(u, core, chip):
+        return starts[u] + core * (sizes[u] // 2) + chip * (sizes[u] // groups)
+
+    def core_half(u, core):
+        return span(rows_of(u, core, 0), sizes[u] // 2)
+
+    def part_of(u, core, chip):
+        return span(rows_of(u, core, chip), sizes[u] // groups)
+
+    def chip_part(u, chip):
+        return span(starts[u] // 2 + chip * (sizes[u] // groups), sizes[u] // groups)
+
+    def core_copy(e, u):
+        return remote(
+            parts.at[e, core_half(u, 1 - c)], from_core.at[e, pl.ds(starts[u] // 2, sizes[u] // 2)],
+            c_send, c_recv.at[e, u], {"aa": core_mate},
+        )
+
+    def chip_copy(e, u):
+        return remote(
+            parts.at[e, part_of(u, c, 1 - x)],
+            from_chip.at[e, pl.ds(starts[u] // groups, sizes[u] // groups)],
+            p_send, p_recv.at[e, u], {"aa": chip_mate},
+        )
+
+    def share_copy(e, u, step):
+        block = gram.at[e, part_of(u, c, 1 - x if step == 2 else x)]
+        return remote(
+            block, block, s_send.at[step], s_recv.at[e, u, min(step, 1)],
             {"aa": chip_mate if step == 0 else core_mate},
         )
 
-    def gram_partial(e, h):
+    def gram_partial(e, u):
+        h = min(u, 1)
+        first = starts[u] - h * wide
+
         @pl.loop(0, 2)
         def _(q):
-            parts[e, h, :, span(q * wide, wide)] = inner_rows(panel[e, h], panel[0, q])
-
-        core_copy(e, h).start()
-
-    def core_sum(e, h):
-        core_copy(e, h).wait_recv()
-        parts[e, h, span(theirs, share)] += from_core[e, h, span((1 - x) * share, share)]
-        chip_copy(e, h).start()
-        parts[e, h, span(mine, share)] += from_core[e, h, span(x * share, share)]
-
-    def gram_share(e, h):
-        chip_copy(e, h).wait_recv()
-        gram[e, span(h * wide + mine, share)] = (
-            parts[e, h, span(mine, share)] + from_chip[e, h]
+            parts[e, pl.ds(starts[u], sizes[u]), pl.ds(pl.multiple_of(q * wide, wide), wide)] = (
+                inner_rows(panel[e, h, :, first : first + sizes[u]], panel[0, q])
+            )
+
+        core_copy(e, u).start()
+
+    def core_sum(e, u):
+        core_copy(e, u).wait_recv()
+        parts[e, part_of(u, c, 1 - x)] += from_core[e, chip_part(u, 1 - x)]
+        chip_copy(e, u).start()
+        parts[e, part_of(u, c, x)] += from_core[e, chip_part(u, x)]
+
+    def gram_share(e, u):
+        chip_copy(e, u).wait_recv()
+        gram[e, part_of(u, c, x)] = (
+            parts[e, part_of(u, c, x)]
+            + from_chip[e, pl.ds(starts[u] // groups, sizes[u] // groups)]
         ).astype(jnp.bfloat16)
-        share_copy(e, h, 0).start()
-        share_copy(e, h, 1).start()
-
-    def relay(e, h):
-        share_copy(e, h, 0).wait_recv()
-        share_copy(e, h, 2).start()
-
-    def gram_ready(e, h):
-        block = gram.at[e, span(h * wide + (1 - c) * core_rows, core_rows)]
+        share_copy(e, u, 0).start()
+        share_copy(e, u, 1).start()
+
+    def relay(e, u):
+        share_copy(e, u, 0).wait_recv()
+        share_copy(e, u, 2).start()
+
+    def gram_ready(e, u):
+        block = gram.at[e, core_half(u, 1 - c)]
         remote(
-            block, block, s_send.at[1], s_recv.at[e, h, 1], {"aa": core_mate}
+            block, block, s_send.at[1], s_recv.at[e, u, 1], {"aa": core_mate}
         ).wait_recv()
 
     def accumulate(held, e, halves, first, start, count):
@@ -315,71 +352,75 @@
                 total[part, :] += term
 
     last = n - 1
-    steps = [[(0, h) for h in range(2)]]
+    events = [(0, (0,), [(0, u) for u in range(3)])]
     for s in range(1, middle + 1):
-        for h in range(2):
-            steps.append([(2 * s - 1, h), (2 * s, h)] if s < middle else [(last, h)])
-    final = len(steps) - 1
+        blocks = [2 * s - 1, 2 * s] if s < middle else [last]
+        for u, group in enumerate(((0, 1), (2,), (3,))):
+            events.append((s, group, [(e, u) for e in blocks]))
+    final = len(events) - 1
 
     def each(do, i):
-        for unit in steps[i]:
-            do(*unit)
-
+        if i >= 0:
+            for unit in events[i][2]:
+                do(*unit)
+
+    def first_power(e):
+        for u in range(3):
+            gram_ready(e, u)
+        accumulate(panel, e, (0, 1), e == 0, 0, rows)
+
+    early = {final - 2: (0, 1, 2), final - 1: (3,), final: (4,)}
     each(gram_partial, 0)
     for i in range(1, final + 1):
-        s, h = (i + 1) // 2, (i + 1) % 2
-        for k in range(2):
-            for d in range(2):
-                if goes(True, d, s, h, k):
-                    pass_on(*ring_x, d, s, h, k)
-            if k == 0 and 1 < i < final - 1:
-                each(gram_share, i - 1)
+        s, group, units = events[i]
+        for e in early.get(i, ()):
+            first_power(e)
+        pass_x(s, group[0])
+        if i > 1:
+            each(gram_share, i - 1)
+        for p in group[1:]:
+            pass_x(s, p)
         if i == 1:
             each(core_sum, 0)
         each(gram_partial, i)
         if i == 2:
             each(gram_share, 0)
-        each(core_sum, i)
         if i == 3:
             each(relay, 0)
-        if 1 < i < final - 1:
-            each(relay, i - 1)
-        if i == final - 1:
-            each(gram_share, i - 1)
-    each(relay, final - 2)
-    each(gram_share, final - 1)
-    for e in range(n):
-        if e == 4:
-            each(gram_share, final)
-        if e == 5:
-            each(relay, final - 1)
-        for h in range(2 if e < last else 1):
-            gram_ready(e, h)
-        accumulate(panel, e, (0, 1) if e < last else (0,), e == 0, 0, rows)
-    relay(last, 1)
+        if i > 2:
+            each(relay, i - 2)
+        each(core_sum, i)
+    first_power(5)
+    first_power(6)
+    each(gram_share, final)
+    each(relay, final - 1)
+    gram_ready(last, 0)
+    accumulate(panel, last, (0,), False, 0, rows)
+    each(relay, final)
     gram_ready(last, 1)
-
-    ring_p = (powers, y_send, y_recv, False)
+    gram_ready(last, 2)
+
     for k in range(2):
         part = pl.ds(k * half, half)
         accumulate(panel, last, (1,), False, k * half, half)
         for h in range(2):
             powers[0, h, part, :] = total[part, h * wide : (h + 1) * wide].astype(jnp.bfloat16)
             for d in range(2):
-                hop(*ring_p, d, 1, h, k).start()
+                hop_p(d, 1, h, k).start()
 
     accumulate(powers, 0, (0, 1), True, 0, rows)
     for s in range(1, middle):
-        for h, k in by_halves:
-            for d in range(2):
-                pass_on(*ring_p, d, s, h, k)
+        for k in range(2):
+            for h in range(2):
+                for d in range(2):
+                    pass_p(d, s, h, k)
         for e in (2 * s - 1, 2 * s):
             accumulate(powers, e, (0, 1), False, 0, rows)
 
     rate = step_ref[()] * factor
     for k in range(2):
         for d in range(2):
-            pass_on(*ring_p, d, middle, d, k)
+            pass_p(d, middle, d, k)
         accumulate(powers, last, (0, 1), False, k * half, half)
         part = pl.ds(k * half, half)
         for h in range(2):
@@ -392,7 +433,7 @@
             weight[part, columns] = weight[part, columns] - rate * direction
 
     def sent(block, send):
-        remote(block, block, send, x_recv.at[0, 0, 0, 0], {"aa": core_mate}).wait_send()
+        remote(block, block, send, x_recv.at[0, 0, 0], {"aa": core_mate}).wait_send()
 
     sent(panel.at[pl.ds(1, n - 1)], x_send)
     sent(powers.at[pl.ds(1, n - 1)], y_send)
@@ -429,8 +470,7 @@
     vmem = pl.BlockSpec(memory_space=pltpu.VMEM)
     hbm = pl.BlockSpec(memory_space=pltpu.HBM)
     smem = pl.BlockSpec(memory_space=pltpu.SMEM)
-    ring = dma((2, middle, 2, 2))
-    units = dma((n, 2))
+    units = dma((n, 3))
     return pl.pallas_call(
         functools.partial(step_kernel, n, groups, 0.2 * math.sqrt(max(ROWS, COLS))),
         out_shape=(
@@ -447,16 +487,16 @@
             pltpu.VMEM((n, 2, rows, wide), jnp.bfloat16),
             pltpu.VMEM((n, 2, rows, wide), jnp.bfloat16),
             pltpu.VMEM((n, width, width), jnp.bfloat16),
-            pltpu.VMEM((n, 2, wide, width), jnp.float32),
-            pltpu.VMEM((n, 2, wide // 2, width), jnp.float32),
-            pltpu.VMEM((n, 2, wide // groups, width), jnp.float32),
+            pltpu.VMEM((n, width, width), jnp.float32),
+            pltpu.VMEM((n, width // 2, width), jnp.float32),
+            pltpu.VMEM((n, width // groups, width), jnp.float32),
             pltpu.VMEM((rows, width), jnp.float32),
             dma((2, n // 2)), dma((n // 2, pieces)),
             dma((5,)), dma((2, groups, pieces)), dma((2, pieces)),
             dma((3,)), dma((3,)),
-            dma, ring, dma, ring,
+            dma, dma((2, middle, 4)), dma, dma((2, middle, 2, 2)),
             dma, units, dma, units,
-            dma((3,)), dma((n, 2, 2)),
+            dma((3,)), dma((n, 3, 2)),
             dma((4,)),
         ],
         compiler_params=pltpu.CompilerParams(
@@ -506,8 +546,7 @@
     tokens, features = activations.shape
     fits = (
         groups == 4 and n == 2 * groups and rows == 2 * features
-        and features % 16 == 0 and tokens % 128 == 0 and width % 256 == 0
-        and width % (32 * groups) == 0
+        and features % 16 == 0 and tokens % 128 == 0 and width % 512 == 0
         and 4 * n * rows * width + 9 * n * width * width + 17 * rows * width < 56 * 2**20
     )
     if fits:

time: 219 us -> 232 us (1.059)
  Pallas kernels: 213 us -> 226 us
    pallas_call x1, Pallas kernels: 213 us -> 226 us  [fused_step(): pl.pallas_call(functools.partial(step_kernel, n, groups, 0.2 * math.sqrt(...]
where the time goes in v5:
time: 232 us; the launch traced here: 231 us
  Pallas kernels  226 us (97%)
  local copies, waits for them, and re-layouts  2.68 us (1%)
    pallas_call x1, Pallas kernels, fused_step(): pl.pallas_call(functools.partial(step_kernel, n, groups, 0.2 * math.sqrt(...  226 us

profile of v5, /device:TPU:0, one launch (start us, length us, event | category | flops | bytes accessed | tf_op | source)
XLA Modules:
  0.0 230.6 jit_solution(14041505557776847115)
XLA Ops:
  1.9 226.0 %step.1 = (f32[1056,512]{1,0:T(8,128)S(1)}, f32[1056,512]{1,0:T(8,128)S(1)}) custom-call(bf16[528,256]{1,0:T(8,128)(2,1)} %bitcast.1, bf16[256,512]{1,0:T(8,128)(2,1)} %grad_hbm.1, f32[1056,512]{1,0:T(8,128)} %momentum_hbm.1, f32[1056,512]{1,0:T(8,128)} %weight_hbm.1, f32[]{:T(128)S(6)} %copy.10.scale_ref, f32[]{:T(128)S(6)} %copy.11.step_ref), custom_call_target="tpu_custom_call" | custom-call | tf_op jit(solution)/shard_map/step/pallas_call | solution.py:474
  228.0 1.3 copy.12
  229.3 1.3 copy.13

commit v6 on v4

--- a/solution.py
+++ b/solution.py
@@ -188,7 +188,6 @@
     loads[3].wait()
 
     by_columns = [(h, k) for h in range(2) for k in range(2)]
-    by_halves = [(h, k) for k in range(2) for h in range(2)]
 
     def row_half(position, k):
         position = (position + n) % n
@@ -248,54 +247,72 @@
 
     mine, theirs = c * core_rows + x * share, c * core_rows + (1 - x) * share
 
-    def core_copy(e, h):
-        return remote(
-            parts.at[e, h, span((1 - c) * core_rows, core_rows)], from_core.at[e, h],
-            c_send, c_recv.at[e, h], {"aa": core_mate},
-        )
-
-    def chip_copy(e, h):
-        return remote(
-            parts.at[e, h, span(theirs, share)], from_chip.at[e, h],
-            p_send, p_recv.at[e, h], {"aa": chip_mate},
-        )
-
-    def share_copy(e, h, step):
-        block = gram.at[e, span(h * wide + (theirs if step == 2 else mine), share)]
-        return remote(
-            block, block, s_send.at[step], s_recv.at[e, h, min(step, 1)],
+    last = n - 1
+    halved = [(last - 2, 1), (last - 1, 1), (last, 0), (last, 1)]
+
+    def slot(e, h, q):
+        return (n + halved.index((e, h)) // 2, halved.index((e, h)) % 2) if q == 1 else (e, h)
+
+    def columns_of(q):
+        return pl.ds(0, width) if q is None else pl.ds(q * wide, wide)
+
+    def core_copy(e, h, q):
+        return remote(
+            parts.at[e, h, span((1 - c) * core_rows, core_rows), columns_of(q)],
+            from_core.at[e, h, :, columns_of(q)],
+            c_send, c_recv.at[slot(e, h, q)], {"aa": core_mate},
+        )
+
+    def chip_copy(e, h, q):
+        return remote(
+            parts.at[e, h, span(theirs, share), columns_of(q)], from_chip.at[e, h, :, columns_of(q)],
+            p_send, p_recv.at[slot(e, h, q)], {"aa": chip_mate},
+        )
+
+    def share_copy(e, h, q, step):
+        block = gram.at[
+            e, span(h * wide + (theirs if step == 2 else mine), share), columns_of(q)
+        ]
+        return remote(
+            block, block, s_send.at[step], s_recv.at[(*slot(e, h, q), min(step, 1))],
             {"aa": chip_mate if step == 0 else core_mate},
         )
 
-    def gram_partial(e, h):
-        @pl.loop(0, 2)
-        def _(q):
-            parts[e, h, :, span(q * wide, wide)] = inner_rows(panel[e, h], panel[0, q])
-
-        core_copy(e, h).start()
-
-    def core_sum(e, h):
-        core_copy(e, h).wait_recv()
-        parts[e, h, span(theirs, share)] += from_core[e, h, span((1 - x) * share, share)]
-        chip_copy(e, h).start()
-        parts[e, h, span(mine, share)] += from_core[e, h, span(x * share, share)]
-
-    def gram_share(e, h):
-        chip_copy(e, h).wait_recv()
-        gram[e, span(h * wide + mine, share)] = (
-            parts[e, h, span(mine, share)] + from_chip[e, h]
+    def gram_partial(e, h, q):
+        if q is None:
+            @pl.loop(0, 2)
+            def _(r):
+                parts[e, h, :, span(r * wide, wide)] = inner_rows(panel[e, h], panel[0, r])
+        else:
+            parts[e, h, :, columns_of(q)] = inner_rows(panel[e, h], panel[0, q])
+        core_copy(e, h, q).start()
+
+    def core_sum(e, h, q):
+        columns = columns_of(q)
+        core_copy(e, h, q).wait_recv()
+        parts[e, h, span(theirs, share), columns] += (
+            from_core[e, h, span((1 - x) * share, share), columns]
+        )
+        chip_copy(e, h, q).start()
+        parts[e, h, span(mine, share), columns] += from_core[e, h, span(x * share, share), columns]
+
+    def gram_share(e, h, q):
+        columns = columns_of(q)
+        chip_copy(e, h, q).wait_recv()
+        gram[e, span(h * wide + mine, share), columns] = (
+            parts[e, h, span(mine, share), columns] + from_chip[e, h, :, columns]
         ).astype(jnp.bfloat16)
-        share_copy(e, h, 0).start()
-        share_copy(e, h, 1).start()
-
-    def relay(e, h):
-        share_copy(e, h, 0).wait_recv()
-        share_copy(e, h, 2).start()
-
-    def gram_ready(e, h):
-        block = gram.at[e, span(h * wide + (1 - c) * core_rows, core_rows)]
+        share_copy(e, h, q, 0).start()
+        share_copy(e, h, q, 1).start()
+
+    def relay(e, h, q):
+        share_copy(e, h, q, 0).wait_recv()
+        share_copy(e, h, q, 2).start()
+
+    def gram_ready(e, h, q):
+        block = gram.at[e, span(h * wide + (1 - c) * core_rows, core_rows), columns_of(q)]
         remote(
-            block, block, s_send.at[1], s_recv.at[e, h, 1], {"aa": core_mate}
+            block, block, s_send.at[1], s_recv.at[(*slot(e, h, q), 1)], {"aa": core_mate}
         ).wait_recv()
 
     def accumulate(held, e, halves, first, start, count):
@@ -314,63 +331,127 @@
             else:
                 total[part, :] += term
 
-    last = n - 1
-    steps = [[(0, h) for h in range(2)]]
-    for s in range(1, middle + 1):
+    whole = [[(0, h, None) for h in range(2)]]
+    for s in range(1, middle - 1):
         for h in range(2):
-            steps.append([(2 * s - 1, h), (2 * s, h)] if s < middle else [(last, h)])
-    final = len(steps) - 1
-
-    def each(do, i):
-        for unit in steps[i]:
+            whole.append([(e, h, None) for e in (2 * s - 1, 2 * s)])
+    whole.append([(e, 0, None) for e in (last - 2, last - 1)])
+    near, mid, end = (
+        [[(e, h, q) for e, h in group] for q in range(2)]
+        for group in (halved[:2], halved[2:3], halved[3:])
+    )
+
+    def each(do, units):
+        for unit in units:
             do(*unit)
 
-    each(gram_partial, 0)
-    for i in range(1, final + 1):
+    def first_power(e):
+        for h in range(2):
+            gram_ready(e, h, None)
+        accumulate(panel, e, (0, 1), e == 0, 0, rows)
+
+    def add_columns(e, halves, q):
+        columns = slice(q * wide, (q + 1) * wide)
+        for k in range(2):
+            part = pl.ds(k * half, half)
+            total[part, columns] += sum(
+                jnp.dot(
+                    panel[e, h, part, :], gram[e, h * wide : (h + 1) * wide, columns],
+                    preferred_element_type=jnp.float32,
+                )
+                for h in halves
+            )
+
+    def receive(s, h, k):
+        for d in range(2):
+            if goes(True, d, s, h, k):
+                pass_on(*ring_x, d, s, h, k)
+
+    def send_power(q):
+        columns = slice(q * wide, (q + 1) * wide)
+        for k in range(2):
+            part = pl.ds(k * half, half)
+            first_powers = total[part, columns] + jnp.dot(
+                panel[last, 1, part, :], gram[last, wide:, columns],
+                preferred_element_type=jnp.float32,
+            )
+            powers[0, q, part, :] = first_powers.astype(jnp.bfloat16)
+            for d in range(2):
+                hop(*ring_p, d, 1, q, k).start()
+
+    ring_p = (powers, y_send, y_recv, False)
+    each(gram_partial, whole[0])
+    for i in range(1, len(whole)):
         s, h = (i + 1) // 2, (i + 1) % 2
-        for k in range(2):
-            for d in range(2):
-                if goes(True, d, s, h, k):
-                    pass_on(*ring_x, d, s, h, k)
-            if k == 0 and 1 < i < final - 1:
-                each(gram_share, i - 1)
+        receive(s, h, 0)
+        if i > 1:
+            each(gram_share, whole[i - 1])
+        receive(s, h, 1)
         if i == 1:
-            each(core_sum, 0)
-        each(gram_partial, i)
+            each(core_sum, whole[0])
+        each(gram_partial, whole[i])
         if i == 2:
-            each(gram_share, 0)
-        each(core_sum, i)
+            each(gram_share, whole[0])
+        each(core_sum, whole[i])
         if i == 3:
-            each(relay, 0)
-        if 1 < i < final - 1:
-            each(relay, i - 1)
-        if i == final - 1:
-            each(gram_share, i - 1)
-    each(relay, final - 2)
-    each(gram_share, final - 1)
-    for e in range(n):
-        if e == 4:
-            each(gram_share, final)
-        if e == 5:
-            each(relay, final - 1)
-        for h in range(2 if e < last else 1):
-            gram_ready(e, h)
-        accumulate(panel, e, (0, 1) if e < last else (0,), e == 0, 0, rows)
-    relay(last, 1)
-    gram_ready(last, 1)
-
-    ring_p = (powers, y_send, y_recv, False)
+            each(relay, whole[0])
+        if i > 1:
+            each(relay, whole[i - 1])
+
+    receive(middle - 1, 1, 0)
+    each(gram_share, whole[-1])
+    receive(middle - 1, 1, 1)
+    for q in range(2):
+        each(gram_partial, near[q])
+    for q in range(2):
+        each(core_sum, near[q])
+    each(relay, whole[-1])
+    for e in range(4):
+        first_power(e)
     for k in range(2):
-        part = pl.ds(k * half, half)
-        accumulate(panel, last, (1,), False, k * half, half)
-        for h in range(2):
-            powers[0, h, part, :] = total[part, h * wide : (h + 1) * wide].astype(jnp.bfloat16)
-            for d in range(2):
-                hop(*ring_p, d, 1, h, k).start()
+        receive(middle, 0, k)
+    for q in range(2):
+        each(gram_partial, mid[q])
+    each(core_sum, mid[0])
+    each(gram_share, near[0])
+    for k in range(2):
+        receive(middle, 1, k)
+    for q in range(2):
+        each(gram_partial, end[q])
+    each(core_sum, end[0])
+    each(gram_share, mid[0])
+    each(core_sum, mid[1])
+    each(relay, near[0])
+    first_power(4)
+    each(gram_share, end[0])
+    each(gram_share, near[1])
+    each(core_sum, end[1])
+    each(relay, mid[0])
+    for e in (last - 2, last - 1):
+        gram_ready(e, 0, None)
+        gram_ready(e, 1, 0)
+        add_columns(e, (0, 1), 0)
+    gram_ready(last, 0, 0)
+    add_columns(last, (0,), 0)
+    each(relay, end[0])
+    gram_ready(last, 1, 0)
+    send_power(0)
+    each(gram_share, mid[1])
+    each(relay, near[1])
+    each(gram_share, end[1])
+    each(relay, mid[1])
+    for e in (last - 2, last - 1):
+        gram_ready(e, 1, 1)
+        add_columns(e, (0, 1), 1)
+    gram_ready(last, 0, 1)
+    add_columns(last, (0,), 1)
+    each(relay, end[1])
+    gram_ready(last, 1, 1)
+    send_power(1)
 
     accumulate(powers, 0, (0, 1), True, 0, rows)
     for s in range(1, middle):
-        for h, k in by_halves:
+        for h, k in by_columns:
             for d in range(2):
                 pass_on(*ring_p, d, s, h, k)
         for e in (2 * s - 1, 2 * s):
@@ -430,7 +511,7 @@
     hbm = pl.BlockSpec(memory_space=pltpu.HBM)
     smem = pl.BlockSpec(memory_space=pltpu.SMEM)
     ring = dma((2, middle, 2, 2))
-    units = dma((n, 2))
+    units = dma((n + 2, 2))
     return pl.pallas_call(
         functools.partial(step_kernel, n, groups, 0.2 * math.sqrt(max(ROWS, COLS))),
         out_shape=(
@@ -456,7 +537,7 @@
             dma((3,)), dma((3,)),
             dma, ring, dma, ring,
             dma, units, dma, units,
-            dma((3,)), dma((n, 2, 2)),
+            dma((3,)), dma((n + 2, 2, 2)),
             dma((4,)),
         ],
         compiler_params=pltpu.CompilerParams(

time: 219 us -> 214 us (0.977)
  Pallas kernels: 213 us -> 210 us
    pallas_call x1, Pallas kernels: 213 us -> 210 us  [fused_step(): pl.pallas_call(functools.partial(step_kernel, n, groups, 0.2 * math.sqrt(...]
where the time goes in v6:
time: 214 us
  Pallas kernels  210 us (98%)
  local copies, waits for them, and re-layouts  2.68 us (1%)
    pallas_call x1, Pallas kernels, fused_step(): pl.pallas_call(functools.partial(step_kernel, n, groups, 0.2 * math.sqrt(...  210 us

profile of v6, /device:TPU:0, one launch (start us, length us, event | category | flops | bytes accessed | tf_op | source)
XLA Modules:
  0.0 214.3 jit_solution(717457284625554647)
XLA Ops:
  1.9 209.7 %step.1 = (f32[1056,512]{1,0:T(8,128)S(1)}, f32[1056,512]{1,0:T(8,128)S(1)}) custom-call(bf16[528,256]{1,0:T(8,128)(2,1)} %bitcast.1, bf16[256,512]{1,0:T(8,128)(2,1)} %grad_hbm.1, f32[1056,512]{1,0:T(8,128)} %momentum_hbm.1, f32[1056,512]{1,0:T(8,128)} %weight_hbm.1, f32[]{:T(128)S(6)} %copy.10.scale_ref, f32[]{:T(128)S(6)} %copy.11.step_ref), custom_call_target="tpu_custom_call" | custom-call | tf_op jit(solution)/shard_map/step/pallas_call | solution.py:515
  211.6 1.3 copy.12
  212.9 1.3 copy.13

commit v7 on v6

--- a/solution.py
+++ b/solution.py
@@ -501,6 +501,17 @@
                 sent(line.at[layer], z_send.at[side, layer])
 
 
+def store_kernel(weight, momentum, new_weight, new_momentum, sem):
+    copies = [
+        pltpu.make_async_copy(weight, new_weight, sem.at[0]),
+        pltpu.make_async_copy(momentum, new_momentum, sem.at[1]),
+    ]
+    for copy in copies:
+        copy.start()
+    for copy in copies:
+        copy.wait()
+
+
 def fused_step(activations, out_grad, momentum, weight, norm_scale, step_size, n, groups):
     tokens, features = activations.shape
     rows, width = momentum.shape
@@ -512,7 +523,7 @@
     smem = pl.BlockSpec(memory_space=pltpu.SMEM)
     ring = dma((2, middle, 2, 2))
     units = dma((n + 2, 2))
-    return pl.pallas_call(
+    results = pl.pallas_call(
         functools.partial(step_kernel, n, groups, 0.2 * math.sqrt(max(ROWS, COLS))),
         out_shape=(
             jax.ShapeDtypeStruct((rows, width), jnp.float32),
@@ -547,6 +558,18 @@
     )(
         pltpu.with_memory_space_constraint(activations.T, pltpu.HBM),
         pltpu.with_memory_space_constraint(out_grad, pltpu.HBM), momentum, weight, norm_scale, step_size)
+    return pl.pallas_call(
+        store_kernel,
+        out_shape=(
+            jax.ShapeDtypeStruct((rows, width), jnp.float32),
+            jax.ShapeDtypeStruct((rows, width), jnp.float32),
+        ),
+        in_specs=[vmem, vmem],
+        out_specs=(hbm, hbm),
+        scratch_shapes=[dma((2,))],
+        compiler_params=pltpu.CompilerParams(vmem_limit_bytes=8 * 1024 * 1024),
+        name="store",
+    )(*results)
 
 
 def plain_gradient(activations, out_grad):

time: 214 us -> 214 us (level)
  local copies, waits for them, and re-layouts: 2.68 us -> 0 us
    unnamed x2 -> x0, local copies, waits for them, and re-layouts: 2.68 us -> none
where the time goes in v7:
time: 214 us
  Pallas kernels  212 us (99%)
    pallas_call x1, Pallas kernels, fused_step(): pl.pallas_call(functools.partial(step_kernel, n, groups, 0.2 * math.sqrt(...  210 us

profile of v7, /device:TPU:0, one launch (start us, length us, event | category | flops | bytes accessed | tf_op | source)
XLA Modules:
  0.0 213.7 jit_solution(9459490618434736001)
XLA Ops:
  1.9 209.7 %step.1 = (f32[1056,512]{1,0:T(8,128)S(1)}, f32[1056,512]{1,0:T(8,128)S(1)}) custom-call(bf16[528,256]{1,0:T(8,128)(2,1)} %bitcast.1, bf16[256,512]{1,0:T(8,128)(2,1)} %grad_hbm.1, f32[1056,512]{1,0:T(8,128)} %momentum_hbm.1, f32[1056,512]{1,0:T(8,128)} %weight_hbm.1, f32[]{:T(128)S(6)} %copy.8.scale_ref, f32[]{:T(128)S(6)} %copy.9.step_ref), custom_call_target="tpu_custom_call" | custom-call | tf_op jit(solution)/shard_map/step/pallas_call | solution.py:526
  211.6 2.1 store.1
